TPU v7x, 32 devices: a whole 2x2x4 slice. The times are simulated.
32 devices in a mesh: row: 4 (over x, core), col: 2 (over y), dp: 4 (over z).
Axes of the slice: x: 2, y: 2, z: 4, core: 2. Of those that a mesh axis runs over, the one named last changes fastest.
Arguments:
- tokens: bfloat16 [16384, 768], P(('dp', 'col', 'row')), may hold values from -6 to 6
- encoded: bfloat16 [12000, 768], P(('dp', 'col', 'row')), may hold values from -6 to 6
- branch: int32 [8, 4], P(('dp', 'col')), may hold values from 512 to 1024
- cotangent: bfloat16 [16384, 768], P(('dp', 'col', 'row')), may hold values from -6 to 6
- gain_self: float32 [768], replicated, may hold values from 0.5 to 1.5
- self_query: bfloat16 [768, 768], P('col', 'row'), may hold values from -0.21875 to 0.21875
- self_key: bfloat16 [768, 768], P('col', 'row'), may hold values from -0.21875 to 0.21875
- self_value: bfloat16 [768, 768], P('col', 'row'), may hold values from -0.21875 to 0.21875
- self_out: bfloat16 [768, 768], P('row', 'col'), may hold values from -3 to 3
- gain_cross: float32 [768], replicated, may hold values from 0.5 to 1.5
- cross_query: bfloat16 [768, 768], P('col', 'row'), may hold values from -0.21875 to 0.21875
- cross_key: bfloat16 [768, 768], P('col', 'row'), may hold values from -0.21875 to 0.21875
- cross_value: bfloat16 [768, 768], P('col', 'row'), may hold values from -0.21875 to 0.21875
- cross_out: bfloat16 [768, 768], P('row', 'col'), may hold values from -4 to 4
- gain_hidden: float32 [768], replicated, may hold values from 0.5 to 1.5
- hidden_up: bfloat16 [768, 3072], P('col', 'row'), may hold values from -0.21875 to 0.21875
- hidden_down: bfloat16 [3072, 768], P('row', 'col'), may hold values from -0.109375 to 0.109375
- gain_final: float32 [768], replicated, may hold values from 0.5 to 1.5
Outputs:
- layer_out: bfloat16 [16384, 768], P(('dp', 'col', 'row'))
- grad_tokens: float32 [16384, 768], P(('dp', 'col', 'row'))
- grad_encoded: float32 [12000, 768], P(('dp', 'col', 'row'))
- grad_gain_self: float32 [768], replicated
- grad_self_query: float32 [768, 768], P('col', 'row')
- grad_self_key: float32 [768, 768], P('col', 'row')
- grad_self_value: float32 [768, 768], P('col', 'row')
- grad_self_out: float32 [768, 768], P('row', 'col')
- grad_gain_cross: float32 [768], replicated
- grad_cross_query: float32 [768, 768], P('col', 'row')
- grad_cross_key: float32 [768, 768], P('col', 'row')
- grad_cross_value: float32 [768, 768], P('col', 'row')
- grad_cross_out: float32 [768, 768], P('row', 'col')
- grad_gain_hidden: float32 [768], replicated
- grad_hidden_up: float32 [768, 3072], P('col', 'row')
- grad_hidden_down: float32 [3072, 768], P('row', 'col')
- grad_gain_final: float32 [768], replicated
Inputs may be any that keep to these rules, and one draw needn't show every extreme that they name: Continuation j of family f sees the first branch[f, j] prompt positions.
All inputs are finite; a program needn't handle non-finite values.
Results may differ from a plain program's by a relative error of at most 0.025.
Values may be sent and summed in bfloat16 or wider, within the bound.
A program may use at most 192 MiB of HBM per device.

v0:
```python
import functools

import jax
import jax.numpy as jnp
from jax import lax
from jax.experimental import pallas as pl
from jax.experimental.pallas import tpu as pltpu
from jax.sharding import PartitionSpec as P


HEAD_DIM = 64
PROMPT = 1024
CONT = 256
NCONT = 4
PAIR = 2 * HEAD_DIM
LOG2E = 1.4426950408889634

eps = 1e-05
big_neg = -1e30
bf16 = jnp.bfloat16
f32 = jnp.float32


def dot(left, right, contract, dtype=f32):
    out = lax.dot_general(left, right, (contract, ((), ())), preferred_element_type=f32)
    return out.astype(dtype)


def nn(left, right, dtype=f32):
    return dot(left, right, ((1,), (0,)), dtype)


def nt(left, right, dtype=f32):
    return dot(left, right, ((1,), (1,)), dtype)


def tn(left, right, dtype=f32):
    return dot(left, right, ((0,), (0,)), dtype)


def unit_rows(rows_in):
    average = jnp.mean(rows_in, axis=-1, keepdims=True)
    centred = rows_in - average
    variance = jnp.mean(centred * centred, axis=-1, keepdims=True)
    scale = lax.rsqrt(variance + eps)
    return centred * scale, scale


def norm_back(unit, scale, gain, upstream):
    cw = upstream * gain
    first = jnp.mean(cw, axis=-1, keepdims=True)
    second = jnp.mean(cw * unit, axis=-1, keepdims=True)
    return scale * (cw - first - unit * second)


def head_masks(rows):
    lane = lax.broadcasted_iota(jnp.int32, (rows, PAIR), 1)
    return (lane < HEAD_DIM, lane >= HEAD_DIM)


def masked_scores(q, keys, limits):
    out = []
    for k, limit in zip(keys, limits):
        s = nt(q, k) * LOG2E
        if limit is not None:
            where, bound = limit
            s = jnp.where(where < bound, s, big_neg)
        out.append(s)
    return out


def fwd_body(q_ref, kv_refs, limits, o_ref, lse_ref):
    rows = q_ref.shape[0]
    masks = head_masks(rows)
    q = q_ref[...] * jnp.asarray(HEAD_DIM**-0.5, bf16)
    keys = [k[...] for k, _ in kv_refs]
    values = [v[...] for _, v in kv_refs]
    blended, logs = [], []
    for mask in masks:
        scores = masked_scores(jnp.where(mask, q, 0), keys, limits)
        top = functools.reduce(
            jnp.maximum, [jnp.max(s, axis=-1, keepdims=True) for s in scores]
        )
        raised = [jnp.exp2(s - top) for s in scores]
        total = functools.reduce(
            jnp.add, [jnp.sum(p, axis=-1, keepdims=True) for p in raised]
        )
        mixed = functools.reduce(
            jnp.add, [nn(p.astype(bf16), v) for p, v in zip(raised, values)]
        )
        blended.append(mixed / total)
        logs.append(top + jnp.log2(total))
    o_ref[...] = jnp.where(masks[0], blended[0], blended[1]).astype(bf16)
    lse_ref[...] = jnp.where(masks[0], logs[0], logs[1])


def bwd_body(q_ref, do_ref, o_ref, lse_ref, kv_refs, limits, dq_ref):
    rows = q_ref.shape[0]
    masks = head_masks(rows)
    q = q_ref[...] * jnp.asarray(HEAD_DIM**-0.5, bf16)
    grad = do_ref[...]
    product = grad.astype(f32) * o_ref[...].astype(f32)
    lse = lse_ref[...]
    keys = [k[...] for k, _ in kv_refs]
    values = [v[...] for _, v in kv_refs]
    sums_k = [None] * len(keys)
    sums_v = [None] * len(keys)
    grads_q = []
    for h, mask in enumerate(masks):
        qh = jnp.where(mask, q, 0)
        gh = jnp.where(mask, grad, 0)
        delta = jnp.sum(jnp.where(mask, product, 0), axis=-1, keepdims=True)
        level = lse[:, h * HEAD_DIM : h * HEAD_DIM + 1]
        scores = masked_scores(qh, keys, limits)
        grad_q = None
        for i, s in enumerate(scores):
            p = jnp.exp2(s - level)
            through = nt(gh, values[i])
            slope = (p * (through - delta)).astype(bf16)
            part = nn(slope, keys[i])
            grad_q = part if grad_q is None else grad_q + part
            dk, dv = tn(qh, slope), tn(gh, p.astype(bf16))
            sums_k[i] = dk if sums_k[i] is None else sums_k[i] + dk
            sums_v[i] = dv if sums_v[i] is None else sums_v[i] + dv
        grads_q.append(grad_q)
    mixed = jnp.where(masks[0], grads_q[0], grads_q[1]) * HEAD_DIM**-0.5
    dq_ref[...] = mixed.astype(bf16)
    return sums_k, sums_v


def self_fwd_kernel(q_ref, kc_ref, vc_ref, ko_ref, vo_ref, at_ref, lim_ref, o_ref, lse_ref):
    lim = lim_ref[...]
    own = lax.broadcasted_iota(jnp.int32, (1, ko_ref.shape[0]), 1)
    limits = [(at_ref[...], lim[:, 0:1]), (own, lim[:, 1:2])]
    fwd_body(q_ref, [(kc_ref, vc_ref), (ko_ref, vo_ref)], limits, o_ref, lse_ref)


def cross_fwd_kernel(q_ref, k_ref, v_ref, at_ref, o_ref, lse_ref, *, frames):
    limits = [(at_ref[...], frames)]
    fwd_body(q_ref, [(k_ref, v_ref)], limits, o_ref, lse_ref)


def self_bwd_kernel(
    q_ref, do_ref, o_ref, lse_ref, kc_ref, vc_ref, ko_ref, vo_ref, at_ref, lim_ref,
    dq_ref, dk_ref, dv_ref, dk_acc, dv_acc,
):
    step = pl.program_id(1)
    last = pl.num_programs(1) - 1
    ctx = kc_ref.shape[0]
    block = ko_ref.shape[0]
    lim = lim_ref[...]
    own = lax.broadcasted_iota(jnp.int32, (1, block), 1)
    limits = [(at_ref[...], lim[:, 0:1]), (own, lim[:, 1:2])]
    sums_k, sums_v = bwd_body(
        q_ref, do_ref, o_ref, lse_ref, [(kc_ref, vc_ref), (ko_ref, vo_ref)], limits, dq_ref
    )
    at = pl.multiple_of(ctx + step * block, block)
    dk_ref[pl.ds(at, block), :] = sums_k[1].T.astype(bf16)
    dv_ref[pl.ds(at, block), :] = sums_v[1].T.astype(bf16)

    @pl.when(step == 0)
    def _():
        dk_acc[...] = sums_k[0]
        dv_acc[...] = sums_v[0]

    @pl.when(step > 0)
    def _():
        dk_acc[...] += sums_k[0]
        dv_acc[...] += sums_v[0]

    @pl.when(step == last)
    def _():
        dk_ref[0:ctx, :] = dk_acc[...].T.astype(bf16)
        dv_ref[0:ctx, :] = dv_acc[...].T.astype(bf16)


def cross_bwd_kernel(
    q_ref, do_ref, o_ref, lse_ref, k_ref, v_ref, at_ref,
    dq_ref, dk_ref, dv_ref, dk_acc, dv_acc, *, frames,
):
    step = pl.program_id(1)
    last = pl.num_programs(1) - 1
    sums_k, sums_v = bwd_body(
        q_ref, do_ref, o_ref, lse_ref, [(k_ref, v_ref)], [(at_ref[...], frames)], dq_ref
    )

    @pl.when(step == 0)
    def _():
        dk_acc[...] = sums_k[0]
        dv_acc[...] = sums_v[0]

    @pl.when(step > 0)
    def _():
        dk_acc[...] += sums_k[0]
        dv_acc[...] += sums_v[0]

    @pl.when(step == last)
    def _():
        dk_ref[...] = dk_acc[...].T.astype(bf16)
        dv_ref[...] = dv_acc[...].T.astype(bf16)


def params():
    return pltpu.CompilerParams(
        dimension_semantics=("arbitrary", "arbitrary"), vmem_limit_bytes=56 * 2**20
    )


def cost(rows, keys, width, matmuls):
    return pl.CostEstimate(
        flops=2 * matmuls * rows * keys * width * 4,
        transcendentals=rows * keys * width // HEAD_DIM,
        bytes_accessed=2 * width * (4 * rows + 4 * keys),
    )


def in_parts(kernel, parts, width, ins, specs, out_specs, shapes, scratch, grid_rows, estimate):
    pairs = width // PAIR
    step = pairs // parts
    outs = None
    for i in range(parts):
        first = i * step

        def moved(spec, first=first):
            if spec is None:
                return pl.BlockSpec(memory_space=pl.ANY)
            block, index = spec
            return pl.BlockSpec(block, lambda p, b: index(p + first, b))

        given = list(ins) + (list(outs) if outs else [])
        extra = len(outs) if outs else 0

        def body(*refs, extra=extra):
            kernel(*refs[: len(ins)], *refs[len(ins) + extra :])

        outs = pl.pallas_call(
            body,
            grid=(step, grid_rows),
            in_specs=[moved(spec) for spec in specs] + [moved(None)] * extra,
            out_specs=[moved(spec) for spec in out_specs],
            out_shape=shapes,
            scratch_shapes=scratch,
            input_output_aliases={len(ins) + j: j for j in range(extra)},
            compiler_params=params(),
            cost_estimate=estimate(width // parts),
        )(*given)
    return outs


def q_spec(block):
    return ((block, PAIR), lambda p, b: (b, p))


def sds(rows, width, kind):
    return jax.ShapeDtypeStruct((rows, width), kind)


def self_specs(ctx):
    first = ctx // CONT
    context = ((ctx, PAIR), lambda p, b: (0, p))
    own = ((CONT, PAIR), lambda p, b: (first + b, p))
    return [
        context, context, own, own,
        ((1, ctx), lambda p, b: (0, 0)),
        ((CONT, 2), lambda p, b: (b, 0)),
    ]


def self_attention(q, k, v, at, lim, parts):
    rows, width = q.shape
    ctx = k.shape[0] - rows
    return in_parts(
        self_fwd_kernel, parts, width,
        (q, k, v, k, v, at, lim), [q_spec(CONT)] + self_specs(ctx),
        [q_spec(CONT)] * 2, [sds(rows, width, bf16), sds(rows, width, f32)], [],
        rows // CONT, lambda w: cost(rows, ctx + CONT, w, 2),
    )


def self_attention_back(q, do, o, lse, k, v, at, lim, parts):
    rows, width = q.shape
    ctx = k.shape[0] - rows
    whole = ((ctx + rows, PAIR), lambda p, b: (0, p))
    return in_parts(
        self_bwd_kernel, parts, width,
        (q, do, o, lse, k, v, k, v, at, lim), [q_spec(CONT)] * 4 + self_specs(ctx),
        [q_spec(CONT), whole, whole],
        [sds(rows, width, bf16), sds(ctx + rows, width, bf16), sds(ctx + rows, width, bf16)],
        [pltpu.VMEM((PAIR, ctx), f32), pltpu.VMEM((PAIR, ctx), f32)],
        rows // CONT, lambda w: cost(rows, ctx + CONT, w, 5),
    )


def cross_attention(q, k, v, at, frames, parts):
    rows, width = q.shape
    keys = k.shape[0]
    whole = ((keys, PAIR), lambda p, b: (0, p))
    return in_parts(
        functools.partial(cross_fwd_kernel, frames=frames), parts, width,
        (q, k, v, at), [q_spec(CONT), whole, whole, ((1, keys), lambda p, b: (0, 0))],
        [q_spec(CONT)] * 2, [sds(rows, width, bf16), sds(rows, width, f32)], [],
        rows // CONT, lambda w: cost(rows, keys, w, 2),
    )


def cross_attention_back(q, do, o, lse, k, v, at, frames, parts):
    rows, width = q.shape
    keys = k.shape[0]
    whole = ((keys, PAIR), lambda p, b: (0, p))
    return in_parts(
        functools.partial(cross_bwd_kernel, frames=frames), parts, width,
        (q, do, o, lse, k, v, at),
        [q_spec(CONT)] * 4 + [whole, whole, ((1, keys), lambda p, b: (0, 0))],
        [q_spec(CONT), whole, whole],
        [sds(rows, width, bf16), sds(keys, width, bf16), sds(keys, width, bf16)],
        [pltpu.VMEM((PAIR, keys), f32), pltpu.VMEM((PAIR, keys), f32)],
        rows // CONT, lambda w: cost(rows, keys, w, 5),
    )


def flip(value, axis, bit):
    size = lax.axis_size(axis)
    return lax.ppermute(value, axis, [(i, i ^ bit) for i in range(size)])


def bits(axis):
    size = lax.axis_size(axis)
    return [1 << b for b in range(size.bit_length() - 1)]


def settle(value):
    return lax.optimization_barrier(value)


def pack_kernel(turned, *refs):
    out, at = refs[-1], 0
    for ref, turn in zip(refs[:-1], turned):
        value = ref[...]
        if turn:
            value = value.astype(f32).T.astype(bf16)
        out[at : at + value.shape[0], :] = value
        at += value.shape[0]


def pack(weights, turned):
    rows = sum(w.shape[1] if t else w.shape[0] for w, t in zip(weights, turned))
    width = weights[0].shape[0] if turned[0] else weights[0].shape[1]
    if width % 128:
        return jnp.concatenate([w.T if t else w for w, t in zip(weights, turned)])
    return pl.pallas_call(
        functools.partial(pack_kernel, turned),
        out_shape=sds(rows, width, bf16),
        grid=(1,),
        in_specs=[pl.BlockSpec(w.shape, lambda i: (0, 0)) for w in weights],
        out_specs=pl.BlockSpec((rows, width), lambda i: (0, 0)),
        compiler_params=pltpu.CompilerParams(vmem_limit_bytes=16 * 2**20),
        cost_estimate=pl.CostEstimate(flops=0, transcendentals=0, bytes_accessed=4 * rows * width),
        name="pack",
    )(*weights)


def col_order(parts):
    count = len(parts)
    place = lax.axis_index("col")
    if count == 1:
        return parts
    if count == 2:
        even = place == 0
        return [jnp.where(even, parts[0], parts[1]), jnp.where(even, parts[1], parts[0])]
    stacked = jnp.stack(parts)
    return [stacked[jnp.bitwise_xor(place, a)] for a in range(count)]


def near_blocks(shard):
    near = [[shard], [flip(shard, "row", 2)]]
    for bit in bits("col"):
        near = [list(p) + [flip(block, "col", bit) for block in p] for p in near]
    return near


def spread_kernel(r, count, plain, *refs):
    sources = refs[: 4 + len(plain)]
    outs = refs[4 + len(plain) : 4 + len(plain) + count + (1 if plain else 0)]
    rest = refs[4 + len(plain) + count + (1 if plain else 0) :]
    buffers, (in_sem, out_sem, send_sem, recv_sem) = rest[:-4], rest[-4:]
    width = sources[0].shape[1]
    me = lax.axis_index("row")
    partner = {"row": me + 1 - 2 * lax.rem(me, 2)}
    place = lax.axis_index("col")

    barrier = pltpu.get_barrier_semaphore()
    pl.semaphore_signal(barrier, inc=1, device_id=partner, device_id_type=pl.DeviceIdType.MESH)
    loads = []
    for i, source in enumerate(sources):
        buffer = buffers[0].at[i] if i < 4 else buffers[1].at[i - 4]
        load = pltpu.make_async_copy(source, buffer, in_sem.at[i])
        load.start()
        loads.append(load)
    pl.semaphore_wait(barrier, 1)
    waits, n = [], 0

    def place_both(piece, here, there):
        nonlocal n
        local_copy = pltpu.make_async_copy(piece, here, out_sem.at[n])
        remote_copy = pltpu.make_async_remote_copy(
            src_ref=piece, dst_ref=there, send_sem=send_sem.at[n], recv_sem=recv_sem.at[n],
            device_id=partner, device_id_type=pl.DeviceIdType.MESH,
        )
        local_copy.start()
        remote_copy.start()
        waits.append((local_copy, remote_copy))
        n += 1

    for i in range(4):
        p, j = i // 2, i % 2
        loads[i].wait()
        side = place if j == 0 else 1 - place
        lanes = pl.ds(pl.multiple_of(side * width, 128), width)
        for w in range(count):
            piece = buffers[0].at[i, pl.ds(w * r, r), :]
            place_both(
                piece,
                outs[w].at[pl.ds(p * r, r), lanes],
                outs[w].at[pl.ds((p + 2) * r, r), lanes],
            )
    for i, rows in enumerate(plain):
        loads[4 + i].wait()
        place_both(
            buffers[1].at[i],
            outs[count].at[pl.ds(i * rows, rows), :],
            outs[count].at[pl.ds((len(plain) + i) * rows, rows), :],
        )
    for local_copy, remote_copy in waits:
        local_copy.wait()
        remote_copy.wait()


def spread(blocks, r, plain, number):
    rows, width = blocks[0][0].shape
    count = rows // r
    if lax.axis_size("col") != 2 or width % 128:
        every = blocks + [[flip(b, "row", 1) for b in p] for p in blocks]
        outs = [
            jnp.concatenate(
                [
                    jnp.concatenate(col_order([b[w * r : (w + 1) * r] for b in p]), axis=1)
                    for p in every
                ]
            )
            for w in range(count)
        ]
        if plain:
            outs.append(jnp.concatenate(list(plain) + [flip(x, "row", 1) for x in plain]))
        return outs
    flat = [b for p in blocks for b in p]
    moves = 4 * count + len(plain)
    shapes = [sds(4 * r, 2 * width, bf16)] * count
    scratch = [pltpu.VMEM((4, rows, width), bf16)]
    if plain:
        n, wide = plain[0].shape
        shapes = shapes + [sds(2 * len(plain) * n, wide, bf16)]
        scratch.append(pltpu.VMEM((len(plain), n, wide), bf16))
    any_place = pl.BlockSpec(memory_space=pl.ANY)
    return pl.pallas_call(
        functools.partial(spread_kernel, r, count, tuple(x.shape[0] for x in plain)),
        out_shape=shapes,
        in_specs=[any_place] * (4 + len(plain)),
        out_specs=[any_place] * len(shapes),
        scratch_shapes=scratch
        + [
            pltpu.SemaphoreType.DMA((4 + len(plain),)),
            pltpu.SemaphoreType.DMA((moves,)),
            pltpu.SemaphoreType.DMA((moves,)),
            pltpu.SemaphoreType.DMA((moves,)),
        ],
        compiler_params=pltpu.CompilerParams(
            collective_id=number, has_side_effects=True, vmem_limit_bytes=24 * 2**20
        ),
        cost_estimate=pl.CostEstimate(flops=0, transcendentals=0, bytes_accessed=24 * rows * width),
    )(*flat, *plain)


def col_halves(value):
    count = lax.axis_size("col")
    width = value.shape[1] // count
    return [value[:, i * width : (i + 1) * width] for i in range(count)]


def add(a, b):
    return (a.astype(f32) + b.astype(f32)).astype(bf16)


def reduce_weights(grads):
    kept = []
    for g in grads:
        half = g.shape[0] // 2
        kept.append(add(g[:half], flip(g[half:], "row", 1)))
    sizes = [k.shape[0] // 2 for k in kept]
    joined = jnp.concatenate(
        [k[:s] for k, s in zip(kept, sizes)] + [k[s:] for k, s in zip(kept, sizes)]
    )
    parts = col_order(col_halves(joined))
    for bit in reversed(bits("col")):
        keep, send = parts[:bit], parts[bit:]
        parts = [add(a, flip(b, "col", bit)) for a, b in zip(keep, send)]
    total = parts[0]
    half = total.shape[0] // 2
    total = settle(add(total[:half], flip(total[half:], "row", 2)))
    for bit in bits("dp")[:-1]:
        total = settle(add(total, flip(total, "dp", bit)))
    last = bits("dp")[-1]
    total = total.astype(f32) + flip(total, "dp", last).astype(f32)
    out, at = [], 0
    for s in sizes:
        out.append(total[at : at + s])
        at += s
    return out


def sum_all(value):
    for axis, bit in [("row", 1), ("col", None), ("row", 2), ("dp", None)]:
        for b in bits(axis) if bit is None else [bit]:
            value = value + flip(value, axis, b)
    return value


def layer(
    tokens,
    encoded,
    branch,
    cotangent,
    gain_self,
    self_query,
    self_key,
    self_value,
    self_out,
    gain_cross,
    cross_query,
    cross_key,
    cross_value,
    cross_out,
    gain_hidden,
    hidden_up,
    hidden_down,
    gain_final,
):
    row = lax.axis_index("row")
    rows, _ = tokens.shape
    frames = encoded.shape[0]
    padded = -(-frames // 128) * 128
    r = self_query.shape[1]
    rf = hidden_up.shape[1]

    blocks_a = near_blocks(pack((self_query, self_key, self_value), (True, True, True)))
    moved = lax.ppermute(tokens, "row", [(0, 2), (1, 3)])
    slot = jnp.where(row < 2, tokens, moved)
    blocks_b = near_blocks(
        pack(
            (self_out, cross_query, cross_key, cross_value, cross_out),
            (False, True, True, True, False),
        ),
    )
    piece = jnp.pad(encoded, ((0, padded - frames), (0, 0)))
    other = flip(piece, "row", 2)
    blocks_c = near_blocks(pack((hidden_up,), (True,)))
    blocks_f = near_blocks(hidden_down)

    position = row * rows + jnp.arange(rows, dtype=jnp.int32)
    chosen = (position - PROMPT) // CONT
    chosen = (chosen[:, None] == jnp.arange(NCONT, dtype=jnp.int32)[None, :]).astype(jnp.int32)
    cut = jnp.sum(chosen * branch[0][None, :], axis=1)
    is_prompt = position < PROMPT
    lim = jnp.stack(
        [
            jnp.where(is_prompt, position + 1, cut),
            jnp.where(is_prompt, 0, position % CONT + 1),
        ],
        axis=1,
    )
    offsets = jnp.arange(rows, dtype=jnp.int32)
    side = jnp.bitwise_and(row, 1)
    at_self = jnp.concatenate([side * rows + offsets, (1 - side) * rows + offsets])[None, :]
    at_cross = (jnp.arange(4 * padded, dtype=jnp.int32) % padded)[None, :]

    w_q, w_k, w_v, context = spread(blocks_a, r, (slot,), 1)
    x = tokens.astype(f32)
    n1, z1 = unit_rows(x)
    a1 = (n1 * gain_self).astype(bf16)
    n1_context = unit_rows(context.astype(f32))[0]
    a1_context = (n1_context * gain_self).astype(bf16)
    a1_all = settle(jnp.concatenate([a1_context, a1]))
    q = nt(a1, w_q, bf16)
    k = nt(a1_all, w_k, bf16)
    v = nt(a1_all, w_v, bf16)
    o, lse = self_attention(q, k, v, at_self, lim, 2)
    w_o, w_cq, w_ck, w_cv, w_co, e = spread(blocks_b, r, (piece, other), 2)
    h1 = x + nn(o, w_o)

    n2, z2 = unit_rows(h1)
    a2 = (n2 * gain_cross).astype(bf16)
    cq = nt(a2, w_cq, bf16)
    ck = nt(e, w_ck, bf16)
    cv = nt(e, w_cv, bf16)
    oc, lse_c = cross_attention(cq, ck, cv, at_cross, frames, 2)
    h2 = h1 + nn(oc, w_co)

    (w_up,) = spread(blocks_c, rf, (), 3)
    (w_down,) = spread(blocks_f, rf, (), 4)
    n3, z3 = unit_rows(h2)
    a3 = (n3 * gain_hidden).astype(bf16)
    u = nt(a3, w_up)
    g = jax.nn.gelu(u, approximate=False).astype(bf16)
    h3 = h2 + nn(g, w_down)
    n4, z4 = unit_rows(h3)
    layer_out = (n4 * gain_final).astype(bf16)

    c3 = cotangent.astype(f32)
    gain_4 = jnp.sum(c3 * n4, axis=0)
    dh3 = norm_back(n4, z4, gain_final, c3)
    db3 = dh3.astype(bf16)
    g_down = tn(g, db3, bf16)
    (s_down,) = reduce_weights([g_down])
    _, gelu_pull = jax.vjp(lambda t: jax.nn.gelu(t, approximate=False), u)
    through = nt(db3, w_down)
    du = gelu_pull(through)[0].astype(bf16)
    g_up = tn(du, a3, bf16)
    (s_up,) = reduce_weights([g_up])
    da3 = nn(du, w_up)
    gain_3 = jnp.sum(da3 * n3, axis=0)
    dh2 = dh3 + norm_back(n3, z3, gain_hidden, da3)
    db2 = dh2.astype(bf16)

    g_co = tn(oc, db2, bf16)
    doc = nt(db2, w_co, bf16)
    dcq, dck, dcv = cross_attention_back(cq, doc, oc, lse_c, ck, cv, at_cross, frames, 3)
    g_cq = tn(dcq, a2, bf16)
    g_ck = tn(dck, e, bf16)
    g_cv = tn(dcv, e, bf16)
    de = (nn(dck, w_ck) + nn(dcv, w_cv)).astype(bf16)
    two = 2 * padded
    de = add(de[:two], flip(de[two:], "row", 1))
    grad_encoded = de[:padded].astype(f32) + flip(de[padded:], "row", 2).astype(f32)
    grad_encoded = grad_encoded[:frames]
    da2 = nn(dcq, w_cq)
    gain_2 = jnp.sum(da2 * n2, axis=0)
    dh1 = dh2 + norm_back(n2, z2, gain_cross, da2)
    db1 = dh1.astype(bf16)

    g_o = tn(o, db1, bf16)
    s_o, s_cq, s_ck, s_cv, s_co = reduce_weights([g_o, g_cq, g_ck, g_cv, g_co])
    do = nt(db1, w_o, bf16)
    dq, dk, dv = self_attention_back(q, do, o, lse, k, v, at_self, lim, 3)
    da_all = nn(dk, w_k) + nn(dv, w_v)
    ctx = PROMPT
    part = da_all[:ctx]
    own = nn(dq, w_q) + da_all[ctx:]
    gain_1 = jnp.sum(own * n1, axis=0) + jnp.sum(part * n1_context, axis=0)
    mine = part[: ctx // 2]
    mine = mine + flip(part[ctx // 2 :].astype(bf16), "row", 1).astype(f32)
    back = lax.ppermute(mine.astype(bf16), "row", [(2, 0), (3, 1)]).astype(f32)
    gains = sum_all(jnp.stack([gain_1, gain_2, gain_3, gain_4]))
    g_q = tn(dq, a1, bf16)
    g_k = tn(dk, a1_all, bf16)
    g_v = tn(dv, a1_all, bf16)
    s_q, s_k, s_v = reduce_weights([g_q, g_k, g_v])
    da1 = own + jnp.where(row < 2, mine + back, 0.0)
    grad_tokens = dh1 + norm_back(n1, z1, gain_self, da1)

    return (
        layer_out,
        grad_tokens,
        grad_encoded,
        gains[0],
        s_q.T,
        s_k.T,
        s_v.T,
        s_o,
        gains[1],
        s_cq.T,
        s_ck.T,
        s_cv.T,
        s_co,
        gains[2],
        s_up.T,
        s_down,
        gains[3],
    )


def solution(mesh):
    rows = P(("dp", "col", "row"), None)
    down, across_ = P("col", "row"), P("row", "col")
    return jax.shard_map(
        layer,
        mesh=mesh,
        in_specs=(
            rows, rows, P(("dp", "col"), None), rows,
            P(), down, down, down, across_,
            P(), down, down, down, across_,
            P(), down, across_, P(),
        ),
        out_specs=(
            rows, rows, rows,
            P(), down, down, down, across_,
            P(), down, down, down, across_,
            P(), down, across_, P(),
        ),
        check_vma=False,
    )
```

profile of v0, /device:TPU:0, one launch (start us, length us, event | category | flops | bytes accessed | tf_op | source)
XLA Modules:
  0.0 594.6 jit_solution(16032334528313528142)
XLA Ops:
  25.1 21.1 %collective-permute-done.3 = bf16[512,768]{1,0:T(8,128)(2,1)} collective-permute-done((bf16[512,768]{1,0:T(8,128)(2,1)}, bf16[512,768]{1,0:T(8,128)(2,1)}, u32[]{:S(2)}, u32[]{:S(2)}) %collective-permute-start.3) | collective-permute-done | bytes 786464 | tf_op jit(solution)/shard_map/ppermute | solution.py:555
  52.1 5.6 shard_map.305
  72.9 8.8 %collective-permute-done.5.refs_2_ = bf16[960,384]{1,0:T(8,128)(2,1)S(1)} collective-permute-done((bf16[960,384]{1,0:T(8,128)(2,1)S(1)}, bf16[960,384]{1,0:T(8,128)(2,1)S(1)}, u32[]{:S(2)}, u32[]{:S(2)}) %collective-permute-start.5) | collective-permute-done | bytes 737312 | tf_op jit(solution)/shard_map/ppermute | solution.py:323
  84.5 10.9 %shard_map.306 = (bf16[512,768]{1,0:T(8,128)(2,1)}, f32[512,768]{1,0:T(8,128)}) custom-call(bf16[512,768]{1,0:T(8,128)(2,1)} %convolution_convert_fusion.17.refs_0_, bf16[1536,768]{1,0:T(8,128)(2,1)} %convolution_convert_fusion.5.refs_1_.refs_3_.refs_4_.refs_6_, bf16[1536,768]{1,0:T(8,128)(2,1)} %convolution_convert_fusion.4.refs_2_.refs_4_.refs_5_.refs_7_, ...), custom_call_target="tpu_custom_call" | custom-call | flops 4026531840 | bytes 5505024 | tf_op jit(solution)/shard_map/pallas_call | solution.py:236
  95.4 11.0 %shard_map.307 = (bf16[512,768]{1,0:T(8,128)(2,1)}, f32[512,768]{1,0:T(8,128)}) custom-call(bf16[512,768]{1,0:T(8,128)(2,1)} %convolution_convert_fusion.17.refs_0_, bf16[1536,768]{1,0:T(8,128)(2,1)} %convolution_convert_fusion.5.refs_1_.refs_3_.refs_4_.refs_6_, ...), custom_call_target="tpu_custom_call", output_to_operand_aliasing={{0}: (7, {}), {1}: (8, {})} | custom-call | flops 4026531840 | bytes 5505024 | tf_op jit(solution)/shard_map/pallas_call | solution.py:236
  112.3 5.7 shard_map.312
  120.2 8.2 %shard_map.308 = (bf16[768,768]{1,0:T(8,128)(2,1)S(1)}, bf16[768,768]{1,0:T(8,128)(2,1)S(1)}, bf16[768,768]{1,0:T(8,128)(2,1)S(1)}, bf16[768,768]{1,0:T(8,128)(2...) custom-call(bf16[960,384]{1,0:T(8,128)(2,1)S(1)} %pack.4.refs_0_, ...), custom_call_target="tpu_custom_call" | custom-call | bytes 8847360 | tf_op jit(solution)/shard_map/pallas_call | solution.py:464
  140.0 11.3 %shard_map.309 = (bf16[512,768]{1,0:T(8,128)(2,1)}, f32[512,768]{1,0:T(8,128)}) custom-call(bf16[512,768]{1,0:T(8,128)(2,1)} %convolution_convert_fusion.16.refs_0_, bf16[1536,768]{1,0:T(8,128)(2,1)} %convolution_convert_fusion.3.refs_1_.refs_4_, bf16[1536,768]{1,0:T(8,128)(2,1)} %convolution_convert_fusion.2.refs_2_.refs_5_, ...), custom_call_target="tpu_custom_call" | custom-call | flops 4831838208 | bytes 6291456 | tf_op jit(solution)/shard_map/pallas_call | solution.py:236
  151.3 11.3 %shard_map.310 = (bf16[512,768]{1,0:T(8,128)(2,1)}, f32[512,768]{1,0:T(8,128)}) custom-call(bf16[512,768]{1,0:T(8,128)(2,1)} %convolution_convert_fusion.16.refs_0_, bf16[1536,768]{1,0:T(8,128)(2,1)} %convolution_convert_fusion.3.refs_1_.refs_4_, ...), custom_call_target="tpu_custom_call", output_to_operand_aliasing={{0}: (4, {}), {1}: (5, {})} | custom-call | flops 4831838208 | bytes 6291456 | tf_op jit(solution)/shard_map/pallas_call | solution.py:236
  165.4 19.7 %multiply_convert_fusion = (bf16[512,3072]{1,0:T(8,128)(2,1)S(1)}, f32[512,3072]{1,0:T(8,128)}, f32[512,3072]{1,0:T(8,128)}) fusion(bf16[3072,768]{1,0:T(8,128)(2,1)S(1)} %shard_map.311, f32[512,768]{1,0:T(8,128)S(1)} %get-tuple-element.191, f32[768]{0:T(1024)S(1)} %copy-done.54, f32[512]{0:T(512)S(1)} %add_rsqrt_fusion.2, f32[512]{0:T(512)S(1)} %broadcast_multiply_fusion.10), kind=kOutput, calls=%fused_computation.3 | convolution fusion | flops 2519728128 | bytes 22027264 | tf_op jit(solution)/shard_map/dot_general | solution.py:25
  189.9 5.1 convolution_convert_fusion
  195.0 7.6 %add_convert_fusion = bf16[512,3072]{1,0:T(8,128)(2,1)S(1)} fusion(f32[512,3072]{1,0:T(8,128)} %get-tuple-element.175, f32[512,3072]{1,0:T(8,128)} %get-tuple-element.192, bf16[3072,768]{1,0:T(8,128)(2,1)S(1)} %bitcast.68, bf16[512,768]{1,0:T(8,128)(2,1)S(1)} %copy-done.31, f32[512,768]{1,0:T(8,128)S(1)} %get-tuple-element.194, ...), kind=kOutput, calls=%fused_computation.2 | convolution fusion | flops 2441478144 | bytes 22817792 | tf_op jit(solution)/shard_map/dot_general | solution.py:25
  214.6 11.6 %shard_map.313 = (bf16[512,768]{1,0:T(8,128)(2,1)}, bf16[1536,768]{1,0:T(8,128)(2,1)}, bf16[1536,768]{1,0:T(8,128)(2,1)}) custom-call(bf16[512,768]{1,0:T(8,128)(2,1)} %convolution_convert_fusion.16.refs_0_, bf16[512,768]{1,0:T(8,128)(2,1)} %convolution_convert_fusion.15.refs_1_, bf16[512,768]{1,0:T(8,128)(2,1)} %get-tuple-element.67.refs_2_, ...), custom_call_target="tpu_custom_call" | custom-call | flops 8053063680 | bytes 4194304 | tf_op jit(solution)/shard_map/pallas_call | solution.py:236
  226.1 12.0 %shard_map.314 = (bf16[512,768]{1,0:T(8,128)(2,1)}, bf16[1536,768]{1,0:T(8,128)(2,1)}, bf16[1536,768]{1,0:T(8,128)(2,1)}) custom-call(bf16[512,768]{1,0:T(8,128)(2,1)} %convolution_convert_fusion.16.refs_0_, bf16[512,768]{1,0:T(8,128)(2,1)} %convolution_convert_fusion.15.refs_1_, ...), custom_call_target="tpu_custom_call", output_to_operand_aliasing={{0}: (7, {}), {1}: (8, {}), {2}: (9, {})} | custom-call | flops 8053063680 | bytes 4194304 | tf_op jit(solution)/shard_map/pallas_call | solution.py:236
  238.2 11.7 %shard_map.315 = (bf16[512,768]{1,0:T(8,128)(2,1)}, bf16[1536,768]{1,0:T(8,128)(2,1)}, bf16[1536,768]{1,0:T(8,128)(2,1)}) custom-call(bf16[512,768]{1,0:T(8,128)(2,1)} %convolution_convert_fusion.16.refs_0_, bf16[512,768]{1,0:T(8,128)(2,1)} %convolution_convert_fusion.15.refs_1_, ...), custom_call_target="tpu_custom_call", output_to_operand_aliasing={{0}: (7, {}), {1}: (8, {}), {2}: (9, {})} | custom-call | flops 8053063680 | bytes 4194304 | tf_op jit(solution)/shard_map/pallas_call | solution.py:236
  265.4 11.8 %shard_map.316 = (bf16[512,768]{1,0:T(8,128)(2,1)}, bf16[1536,768]{1,0:T(8,128)(2,1)}, bf16[1536,768]{1,0:T(8,128)(2,1)}) custom-call(bf16[512,768]{1,0:T(8,128)(2,1)} %convolution_convert_fusion.17.refs_0_, bf16[512,768]{1,0:T(8,128)(2,1)} %convolution_convert_fusion.14.refs_1_, bf16[512,768]{1,0:T(8,128)(2,1)} %get-tuple-element.59.refs_2_, ...), custom_call_target="tpu_custom_call" | custom-call | flops 6710886400 | bytes 3670016 | tf_op jit(solution)/shard_map/pallas_call | solution.py:236
  277.2 12.0 %shard_map.317 = (bf16[512,768]{1,0:T(8,128)(2,1)}, bf16[1536,768]{1,0:T(8,128)(2,1)}, bf16[1536,768]{1,0:T(8,128)(2,1)}) custom-call(bf16[512,768]{1,0:T(8,128)(2,1)} %convolution_convert_fusion.17.refs_0_, bf16[512,768]{1,0:T(8,128)(2,1)} %convolution_convert_fusion.14.refs_1_, ...), custom_call_target="tpu_custom_call", output_to_operand_aliasing={{0}: (10, {}), {1}: (11, {}), {2}: (12, {})} | custom-call | flops 6710886400 | bytes 3670016 | tf_op jit(solution)/shard_map/pallas_call | solution.py:236
  289.2 12.0 %shard_map.318 = (bf16[512,768]{1,0:T(8,128)(2,1)}, bf16[1536,768]{1,0:T(8,128)(2,1)}, bf16[1536,768]{1,0:T(8,128)(2,1)}) custom-call(bf16[512,768]{1,0:T(8,128)(2,1)} %convolution_convert_fusion.17.refs_0_, bf16[512,768]{1,0:T(8,128)(2,1)} %convolution_convert_fusion.14.refs_1_, ...), custom_call_target="tpu_custom_call", output_to_operand_aliasing={{0}: (10, {}), {1}: (11, {}), {2}: (12, {})} | custom-call | flops 6710886400 | bytes 3670016 | tf_op jit(solution)/shard_map/pallas_call | solution.py:236
  305.8 6.0 %fusion.59 = f32[1536,768]{1,0:T(8,128)} fusion(bf16[1536,768]{1,0:T(8,128)(2,1)} %get-tuple-element.86, bf16[768,768]{1,0:T(8,128)(2,1)S(1)} %copy-done.17), kind=kOutput, calls=%fused_computation.213 | convolution fusion | flops 1811939328 | bytes 8257536 | tf_op jit(solution)/shard_map/dot_general | solution.py:25
  322.0 5.3 convolution_add_fusion
  345.4 19.7 %collective-permute-done.15 = bf16[512,768]{1,0:T(8,128)(2,1)S(1)} collective-permute-done((bf16[512,768]{1,0:T(8,128)(2,1)S(1)}, bf16[512,768]{1,0:T(8,128)(2,1)S(1)}, u32[]{:S(2)}, u32[]{:S(2)}) %collective-permute-start.15) | collective-permute-done | bytes 786464 | tf_op jit(solution)/shard_map/ppermute | solution.py:660
  373.9 19.6 %collective-permute-done.20 = f32[4,768]{1,0:T(4,128)S(1)} collective-permute-done((f32[4,768]{1,0:T(4,128)S(1)}, f32[4,768]{1,0:T(4,128)S(1)}, u32[]{:S(2)}, u32[]{:S(2)}) %collective-permute-start.20) | collective-permute-done | bytes 12320 | tf_op jit(solution)/shard_map/ppermute | solution.py:323
  411.0 26.8 %collective-permute-done.35 = bf16[1920,384]{1,0:T(8,128)(2,1)S(1)} collective-permute-done((bf16[1920,384]{1,0:T(8,128)(2,1)S(1)}, bf16[1920,384]{1,0:T(8,128)(2,1)S(1)}, u32[]{:S(2)}, u32[]{:S(2)}) %collective-permute-start.35) | collective-permute-done | bytes 1474592 | tf_op jit(solution)/shard_map/ppermute | solution.py:323
  440.7 22.3 %collective-permute-done.40 = bf16[1536,384]{1,0:T(8,128)(2,1)S(1)} collective-permute-done((bf16[1536,384]{1,0:T(8,128)(2,1)S(1)}, bf16[1536,384]{1,0:T(8,128)(2,1)S(1)}, u32[]{:S(2)}, u32[]{:S(2)}) %collective-permute-start.40) | collective-permute-done | bytes 1179680 | tf_op jit(solution)/shard_map/ppermute | solution.py:323
  463.9 21.7 %collective-permute-done.45 = bf16[1536,384]{1,0:T(8,128)(2,1)S(1)} collective-permute-done((bf16[1536,384]{1,0:T(8,128)(2,1)S(1)}, bf16[1536,384]{1,0:T(8,128)(2,1)S(1)}, u32[]{:S(2)}, u32[]{:S(2)}) %collective-permute-start.45) | collective-permute-done | bytes 1179680 | tf_op jit(solution)/shard_map/ppermute | solution.py:323
  489.4 9.3 %collective-permute-done.46 = bf16[768,384]{1,0:T(8,128)(2,1)S(1)} collective-permute-done((bf16[768,384]{1,0:T(8,128)(2,1)S(1)}, bf16[768,384]{1,0:T(8,128)(2,1)S(1)}, u32[]{:S(2)}, u32[]{:S(2)}) %collective-permute-start.46) | collective-permute-done | bytes 589856 | tf_op jit(solution)/shard_map/ppermute | solution.py:323
  500.5 13.7 %collective-permute-done.37 = bf16[960,384]{1,0:T(8,128)(2,1)S(1)} collective-permute-done((bf16[960,384]{1,0:T(8,128)(2,1)S(1)}, bf16[960,384]{1,0:T(8,128)(2,1)S(1)}, u32[]{:S(2)}, u32[]{:S(2)}) %collective-permute-start.37) | collective-permute-done | bytes 737312 | tf_op jit(solution)/shard_map/ppermute | solution.py:323
  515.5 20.0 %collective-permute-done.42 = bf16[768,384]{1,0:T(8,128)(2,1)S(1)} collective-permute-done((bf16[768,384]{1,0:T(8,128)(2,1)S(1)}, bf16[768,384]{1,0:T(8,128)(2,1)S(1)}, u32[]{:S(2)}, u32[]{:S(2)}) %collective-permute-start.42) | collective-permute-done | bytes 589856 | tf_op jit(solution)/shard_map/ppermute | solution.py:323
  537.6 6.9 %collective-permute-done.47 = bf16[768,384]{1,0:T(8,128)(2,1)S(1)} collective-permute-done((bf16[768,384]{1,0:T(8,128)(2,1)S(1)}, bf16[768,384]{1,0:T(8,128)(2,1)S(1)}, u32[]{:S(2)}, u32[]{:S(2)}) %collective-permute-start.47) | collective-permute-done | bytes 589856 | tf_op jit(solution)/shard_map/ppermute | solution.py:323
  545.8 23.6 %collective-permute-done.38 = bf16[960,384]{1,0:T(8,128)(2,1)S(1)} collective-permute-done((bf16[960,384]{1,0:T(8,128)(2,1)S(1)}, bf16[960,384]{1,0:T(8,128)(2,1)S(1)}, u32[]{:S(2)}, u32[]{:S(2)}) %collective-permute-start.38) | collective-permute-done | bytes 737312 | tf_op jit(solution)/shard_map/ppermute | solution.py:323
  570.6 11.4 %collective-permute-done.43 = bf16[768,384]{1,0:T(8,128)(2,1)S(1)} collective-permute-done((bf16[768,384]{1,0:T(8,128)(2,1)S(1)}, bf16[768,384]{1,0:T(8,128)(2,1)S(1)}, u32[]{:S(2)}, u32[]{:S(2)}) %collective-permute-start.43) | collective-permute-done | bytes 589856 | tf_op jit(solution)/shard_map/ppermute | solution.py:323
  583.5 9.8 %collective-permute-done.48 = bf16[768,384]{1,0:T(8,128)(2,1)S(1)} collective-permute-done((bf16[768,384]{1,0:T(8,128)(2,1)S(1)}, bf16[768,384]{1,0:T(8,128)(2,1)S(1)}, u32[]{:S(2)}, u32[]{:S(2)}) %collective-permute-start.48) | collective-permute-done | bytes 589856 | tf_op jit(solution)/shard_map/ppermute | solution.py:323
  (389 shorter events, 178.8 us)
Async XLA Ops:
  7.2 41.8 %collective-permute-start = (bf16[576,384]{1,0:T(8,128)(2,1)S(1)}, bf16[576,384]{1,0:T(8,128)(2,1)}, u32[]{:S(2)}, u32[]{:S(2)}) collective-permute-start(bf16[576,384]{1,0:T(8,128)(2,1)S(1)} %pack.3.refs_0_), channel_id=1, source_target_pairs={{0,4},{4,0},{1,5},{5,1},{2,6},{6,2},{3,7},{7,3},{8,12},{12,8},{9,1... | collective-permute-start | bytes 1327112 | tf_op jit(solution)/shard_map/ppermute | solution.py:323
  8.9 42.6 %collective-permute-start.9 = (bf16[768,384]{1,0:T(8,128)(2,1)S(1)}, bf16[768,384]{1,0:T(8,128)(2,1)}, u32[]{:S(2)}, u32[]{:S(2)}) collective-permute-start(bf16[768,384]{1,0:T(8,128)(2,1)S(1)} %pack.5.refs_0_), channel_id=1, source_target_pairs={{0,16},{8,24},{16,0},{24,8},{1,17},{9,25},{17,1},{25,9},{2,18},{10... | collective-permute-start | bytes 1769480 | tf_op jit(solution)/shard_map/ppermute | solution.py:323
  9.5 59.9 %collective-permute-start.8 = (bf16[768,384]{1,0:T(8,128)(2,1)S(1)}, bf16[768,384]{1,0:T(8,128)(2,1)}, u32[]{:S(2)}, u32[]{:S(2)}) collective-permute-start(bf16[768,384]{1,0:T(8,128)(2,1)S(1)} %pack.5.refs_0_), channel_id=1, source_target_pairs={{0,4},{4,0},{1,5},{5,1},{2,6},{6,2},{3,7},{7,3},{8,12},{12,8},{9,1... | collective-permute-start | bytes 1769480 | tf_op jit(solution)/shard_map/ppermute | solution.py:323
  9.6 36.6 %collective-permute-start.3 = (bf16[512,768]{1,0:T(8,128)(2,1)}, bf16[512,768]{1,0:T(8,128)(2,1)}, u32[]{:S(2)}, u32[]{:S(2)}) collective-permute-start(bf16[512,768]{1,0:T(8,128)(2,1)} %param.18), channel_id=1, source_target_pairs={{0,16},{8,24},{1,17},{9,25},{2,18},{10,26},{3,19},{11,27},{4,20},{... | collective-permute-start | bytes 2359304 | tf_op jit(solution)/shard_map/ppermute | solution.py:555
  20.4 31.2 %collective-permute-start.2 = (bf16[576,384]{1,0:T(8,128)(2,1)S(1)}, bf16[576,384]{1,0:T(8,128)(2,1)}, u32[]{:S(2)}, u32[]{:S(2)}) collective-permute-start(bf16[576,384]{1,0:T(8,128)(2,1)S(1)} %collective-permute-done.1.refs_2_), channel_id=1, source_target_pairs={{0,4},{4,0},{1,5},{5,1},{2,6},{6,2},{3,7},{7,3},{8,12},{12,8},{9,1... | collective-permute-start | bytes 1327112 | tf_op jit(solution)/shard_map/ppermute | solution.py:323
  46.2 66.1 %collective-permute-start.11 = (bf16[768,384]{1,0:T(8,128)(2,1)}, bf16[768,384]{1,0:T(8,128)(2,1)}, u32[]{:S(2)}, u32[]{:S(2)}) collective-permute-start(bf16[768,384]{1,0:T(8,128)(2,1)} %refs_0_.6), channel_id=1, source_target_pairs={{0,4},{4,0},{1,5},{5,1},{2,6},{6,2},{3,7},{7,3},{8,12},{12,8},{9,1... | collective-permute-start | bytes 1769480 | tf_op jit(solution)/shard_map/ppermute | solution.py:323
  49.0 22.0 %collective-permute-start.12 = (bf16[768,384]{1,0:T(8,128)(2,1)}, bf16[768,384]{1,0:T(8,128)(2,1)}, u32[]{:S(2)}, u32[]{:S(2)}) collective-permute-start(bf16[768,384]{1,0:T(8,128)(2,1)} %refs_0_.6), channel_id=1, source_target_pairs={{0,16},{8,24},{16,0},{24,8},{1,17},{9,25},{17,1},{25,9},{2,18},{10... | collective-permute-start | bytes 1769480 | tf_op jit(solution)/shard_map/ppermute | solution.py:323
  51.5 30.2 %collective-permute-start.5 = (bf16[960,384]{1,0:T(8,128)(2,1)S(1)}, bf16[960,384]{1,0:T(8,128)(2,1)S(1)}, u32[]{:S(2)}, u32[]{:S(2)}) collective-permute-start(bf16[960,384]{1,0:T(8,128)(2,1)S(1)} %pack.4.refs_0_), channel_id=1, source_target_pairs={{0,16},{8,24},{16,0},{24,8},{1,17},{9,25},{17,1},{25,9},{2,18},{10... | collective-permute-start | bytes 2211848 | tf_op jit(solution)/shard_map/ppermute | solution.py:323
  51.6 30.6 %collective-permute-start.10 = (bf16[768,384]{1,0:T(8,128)(2,1)}, bf16[768,384]{1,0:T(8,128)(2,1)S(1)}, u32[]{:S(2)}, u32[]{:S(2)}) collective-permute-start(bf16[768,384]{1,0:T(8,128)(2,1)} %collective-permute-done.9.refs_2_), channel_id=1, source_target_pairs={{0,4},{4,0},{1,5},{5,1},{2,6},{6,2},{3,7},{7,3},{8,12},{12,8},{9,1... | collective-permute-start | bytes 1769480 | tf_op jit(solution)/shard_map/ppermute | solution.py:323
  69.4 50.7 %collective-permute-start.4 = (bf16[960,384]{1,0:T(8,128)(2,1)S(1)}, bf16[960,384]{1,0:T(8,128)(2,1)}, u32[]{:S(2)}, u32[]{:S(2)}) collective-permute-start(bf16[960,384]{1,0:T(8,128)(2,1)S(1)} %pack.4.refs_0_), channel_id=1, source_target_pairs={{0,4},{4,0},{1,5},{5,1},{2,6},{6,2},{3,7},{7,3},{8,12},{12,8},{9,1... | collective-permute-start | bytes 2211848 | tf_op jit(solution)/shard_map/ppermute | solution.py:323
  71.0 49.2 %collective-permute-start.7 = (bf16[384,768]{1,0:T(8,128)(2,1)S(1)}, bf16[384,768]{1,0:T(8,128)(2,1)}, u32[]{:S(2)}, u32[]{:S(2)}) collective-permute-start(bf16[384,768]{1,0:T(8,128)(2,1)S(1)} %pad.4.refs_4_), channel_id=1, source_target_pairs={{0,16},{8,24},{16,0},{24,8},{1,17},{9,25},{17,1},{25,9},{2,18},{10... | collective-permute-start | bytes 1769480 | tf_op jit(solution)/shard_map/ppermute | solution.py:323
  81.7 30.6 %collective-permute-start.13 = (bf16[768,384]{1,0:T(8,128)(2,1)}, bf16[768,384]{1,0:T(8,128)(2,1)}, u32[]{:S(2)}, u32[]{:S(2)}) collective-permute-start(bf16[768,384]{1,0:T(8,128)(2,1)} %collective-permute-done.12.refs_2_), channel_id=1, source_target_pairs={{0,4},{4,0},{1,5},{5,1},{2,6},{6,2},{3,7},{7,3},{8,12},{12,8},{9,1... | collective-permute-start | bytes 1769480 | tf_op jit(solution)/shard_map/ppermute | solution.py:323
  83.0 37.1 %collective-permute-start.6 = (bf16[960,384]{1,0:T(8,128)(2,1)S(1)}, bf16[960,384]{1,0:T(8,128)(2,1)}, u32[]{:S(2)}, u32[]{:S(2)}) collective-permute-start(bf16[960,384]{1,0:T(8,128)(2,1)S(1)} %collective-permute-done.5.refs_2_), channel_id=1, source_target_pairs={{0,4},{4,0},{1,5},{5,1},{2,6},{6,2},{3,7},{7,3},{8,12},{12,8},{9,1... | collective-permute-start | bytes 2211848 | tf_op jit(solution)/shard_map/ppermute | solution.py:323
  311.9 97.0 %collective-permute-start.44 = (bf16[1536,768]{1,0:T(8,128)(2,1)S(1)}, bf16[1536,768]{1,0:T(8,128)(2,1)S(1)}, u32[]{:S(2)}, u32[]{:S(2)}) collective-permute-start(bf16[1536,768]{1,0:T(8,128)(2,1)S(1)} %slice.371), channel_id=1, source_target_pairs={{0,8},{8,0},{16,24},{24,16},{1,9},{9,1},{17,25},{25,17},{2,10},{10... | collective-permute-start | bytes 7077896 | tf_op jit(solution)/shard_map/ppermute | solution.py:323
  332.2 75.2 %collective-permute-start.39 = (bf16[1536,768]{1,0:T(8,128)(2,1)S(1)}, bf16[1536,768]{1,0:T(8,128)(2,1)S(1)}, u32[]{:S(2)}, u32[]{:S(2)}) collective-permute-start(bf16[1536,768]{1,0:T(8,128)(2,1)S(1)} %slice.365), channel_id=1, source_target_pairs={{0,8},{8,0},{16,24},{24,16},{1,9},{9,1},{17,25},{25,17},{2,10},{10... | collective-permute-start | bytes 7077896 | tf_op jit(solution)/shard_map/ppermute | solution.py:323
  342.6 27.7 %collective-permute-start.26 = (bf16[1152,384]{1,0:T(8,128)(2,1)S(1)}, bf16[1152,384]{1,0:T(8,128)(2,1)S(1)}, u32[]{:S(2)}, u32[]{:S(2)}) collective-permute-start(bf16[1152,384]{1,0:T(8,128)(2,1)S(1)} %broadcast_select_fusion.3), channel_id=1, source_target_pairs={{0,4},{4,0},{1,5},{5,1},{2,6},{6,2},{3,7},{7,3},{8,12},{12,8},{9,1... | collective-permute-start | bytes 2654216 | tf_op jit(solution)/shard_map/ppermute | solution.py:323
  343.5 21.6 %collective-permute-start.15 = (bf16[512,768]{1,0:T(8,128)(2,1)S(1)}, bf16[512,768]{1,0:T(8,128)(2,1)S(1)}, u32[]{:S(2)}, u32[]{:S(2)}) collective-permute-start(bf16[512,768]{1,0:T(8,128)(2,1)S(1)} %fusion.33), channel_id=1, source_target_pairs={{16,0},{24,8},{17,1},{25,9},{18,2},{26,10},{19,3},{27,11},{20,4},{... | collective-permute-start | bytes 2359304 | tf_op jit(solution)/shard_map/ppermute | solution.py:660
  368.0 36.5 %collective-permute-start.17 = (bf16[384,768]{1,0:T(8,128)(2,1)S(1)}, bf16[384,768]{1,0:T(8,128)(2,1)S(1)}, u32[]{:S(2)}, u32[]{:S(2)}) collective-permute-start(bf16[384,768]{1,0:T(8,128)(2,1)S(1)} %get-tuple-element.184), channel_id=1, source_target_pairs={{0,16},{8,24},{16,0},{24,8},{1,17},{9,25},{17,1},{25,9},{2,18},{10... | collective-permute-start | bytes 1769480 | tf_op jit(solution)/shard_map/ppermute | solution.py:323
  370.7 34.9 %collective-permute-start.27 = (bf16[576,384]{1,0:T(8,128)(2,1)S(1)}, bf16[576,384]{1,0:T(8,128)(2,1)S(1)}, u32[]{:S(2)}, u32[]{:S(2)}) collective-permute-start(bf16[576,384]{1,0:T(8,128)(2,1)S(1)} %slice.329), channel_id=1, source_target_pairs={{0,16},{8,24},{16,0},{24,8},{1,17},{9,25},{17,1},{25,9},{2,18},{10... | collective-permute-start | bytes 1327112 | tf_op jit(solution)/shard_map/ppermute | solution.py:323
  402.6 35.2 %collective-permute-start.35 = (bf16[1920,384]{1,0:T(8,128)(2,1)S(1)}, bf16[1920,384]{1,0:T(8,128)(2,1)S(1)}, u32[]{:S(2)}, u32[]{:S(2)}) collective-permute-start(bf16[1920,384]{1,0:T(8,128)(2,1)S(1)} %broadcast_select_fusion), channel_id=1, source_target_pairs={{0,4},{4,0},{1,5},{5,1},{2,6},{6,2},{3,7},{7,3},{8,12},{12,8},{9,1... | collective-permute-start | bytes 4423688 | tf_op jit(solution)/shard_map/ppermute | solution.py:323
  405.7 33.0 %collective-permute-start.28 = (bf16[576,384]{1,0:T(8,128)(2,1)S(1)}, bf16[576,384]{1,0:T(8,128)(2,1)S(1)}, u32[]{:S(2)}, u32[]{:S(2)}) collective-permute-start(bf16[576,384]{1,0:T(8,128)(2,1)S(1)} %add_convert_fusion.24), channel_id=1, source_target_pairs={{0,1},{1,0},{2,3},{3,2},{4,5},{5,4},{6,7},{7,6},{8,9},{9,8},{10,11... | collective-permute-start | bytes 1327112 | tf_op jit(solution)/shard_map/ppermute | solution.py:323
  408.1 55.0 %collective-permute-start.40 = (bf16[1536,384]{1,0:T(8,128)(2,1)S(1)}, bf16[1536,384]{1,0:T(8,128)(2,1)S(1)}, u32[]{:S(2)}, u32[]{:S(2)}) collective-permute-start(bf16[1536,384]{1,0:T(8,128)(2,1)S(1)} %broadcast_select_fusion.2), channel_id=1, source_target_pairs={{0,4},{4,0},{1,5},{5,1},{2,6},{6,2},{3,7},{7,3},{8,12},{12,8},{9,1... | collective-permute-start | bytes 3538952 | tf_op jit(solution)/shard_map/ppermute | solution.py:323
  409.7 75.9 %collective-permute-start.45 = (bf16[1536,384]{1,0:T(8,128)(2,1)S(1)}, bf16[1536,384]{1,0:T(8,128)(2,1)S(1)}, u32[]{:S(2)}, u32[]{:S(2)}) collective-permute-start(bf16[1536,384]{1,0:T(8,128)(2,1)S(1)} %broadcast_select_fusion.1), channel_id=1, source_target_pairs={{0,4},{4,0},{1,5},{5,1},{2,6},{6,2},{3,7},{7,3},{8,12},{12,8},{9,1... | collective-permute-start | bytes 3538952 | tf_op jit(solution)/shard_map/ppermute | solution.py:323
  438.4 48.3 %collective-permute-start.36 = (bf16[960,384]{1,0:T(8,128)(2,1)S(1)}, bf16[960,384]{1,0:T(8,128)(2,1)S(1)}, u32[]{:S(2)}, u32[]{:S(2)}) collective-permute-start(bf16[960,384]{1,0:T(8,128)(2,1)S(1)} %slice.356), channel_id=1, source_target_pairs={{0,16},{8,24},{16,0},{24,8},{1,17},{9,25},{17,1},{25,9},{2,18},{10... | collective-permute-start | bytes 2211848 | tf_op jit(solution)/shard_map/ppermute | solution.py:323
  438.9 49.7 %collective-permute-start.29 = (bf16[576,384]{1,0:T(8,128)(2,1)S(1)}, bf16[576,384]{1,0:T(8,128)(2,1)S(1)}, u32[]{:S(2)}, u32[]{:S(2)}) collective-permute-start(bf16[576,384]{1,0:T(8,128)(2,1)S(1)} %add_convert_fusion.23), channel_id=1, source_target_pairs={{0,2},{1,3},{2,0},{3,1},{4,6},{5,7},{6,4},{7,5},{8,10},{9,11},{10,... | collective-permute-start | bytes 1327112 | tf_op jit(solution)/shard_map/ppermute | solution.py:323
  463.6 25.1 %collective-permute-start.41 = (bf16[768,384]{1,0:T(8,128)(2,1)S(1)}, bf16[768,384]{1,0:T(8,128)(2,1)S(1)}, u32[]{:S(2)}, u32[]{:S(2)}) collective-permute-start(bf16[768,384]{1,0:T(8,128)(2,1)S(1)} %slice.369), channel_id=1, source_target_pairs={{0,16},{8,24},{16,0},{24,8},{1,17},{9,25},{17,1},{25,9},{2,18},{10... | collective-permute-start | bytes 1769480 | tf_op jit(solution)/shard_map/ppermute | solution.py:323
  486.9 27.3 %collective-permute-start.37 = (bf16[960,384]{1,0:T(8,128)(2,1)S(1)}, bf16[960,384]{1,0:T(8,128)(2,1)S(1)}, u32[]{:S(2)}, u32[]{:S(2)}) collective-permute-start(bf16[960,384]{1,0:T(8,128)(2,1)S(1)} %add_convert_fusion.10), channel_id=1, source_target_pairs={{0,1},{1,0},{2,3},{3,2},{4,5},{5,4},{6,7},{7,6},{8,9},{9,8},{10,11... | collective-permute-start | bytes 2211848 | tf_op jit(solution)/shard_map/ppermute | solution.py:323
  488.8 46.6 %collective-permute-start.42 = (bf16[768,384]{1,0:T(8,128)(2,1)S(1)}, bf16[768,384]{1,0:T(8,128)(2,1)S(1)}, u32[]{:S(2)}, u32[]{:S(2)}) collective-permute-start(bf16[768,384]{1,0:T(8,128)(2,1)S(1)} %add_convert_fusion.14), channel_id=1, source_target_pairs={{0,1},{1,0},{2,3},{3,2},{4,5},{5,4},{6,7},{7,6},{8,9},{9,8},{10,11... | collective-permute-start | bytes 1769480 | tf_op jit(solution)/shard_map/ppermute | solution.py:323
  498.9 45.6 %collective-permute-start.47 = (bf16[768,384]{1,0:T(8,128)(2,1)S(1)}, bf16[768,384]{1,0:T(8,128)(2,1)S(1)}, u32[]{:S(2)}, u32[]{:S(2)}) collective-permute-start(bf16[768,384]{1,0:T(8,128)(2,1)S(1)} %add_convert_fusion.12), channel_id=1, source_target_pairs={{0,1},{1,0},{2,3},{3,2},{4,5},{5,4},{6,7},{7,6},{8,9},{9,8},{10,11... | collective-permute-start | bytes 1769480 | tf_op jit(solution)/shard_map/ppermute | solution.py:323
  514.4 54.9 %collective-permute-start.38 = (bf16[960,384]{1,0:T(8,128)(2,1)S(1)}, bf16[960,384]{1,0:T(8,128)(2,1)S(1)}, u32[]{:S(2)}, u32[]{:S(2)}) collective-permute-start(bf16[960,384]{1,0:T(8,128)(2,1)S(1)} %add_convert_fusion.9), channel_id=1, source_target_pairs={{0,2},{1,3},{2,0},{3,1},{4,6},{5,7},{6,4},{7,5},{8,10},{9,11},{10,... | collective-permute-start | bytes 2211848 | tf_op jit(solution)/shard_map/ppermute | solution.py:323
  535.6 46.3 %collective-permute-start.43 = (bf16[768,384]{1,0:T(8,128)(2,1)S(1)}, bf16[768,384]{1,0:T(8,128)(2,1)S(1)}, u32[]{:S(2)}, u32[]{:S(2)}) collective-permute-start(bf16[768,384]{1,0:T(8,128)(2,1)S(1)} %add_convert_fusion.13), channel_id=1, source_target_pairs={{0,2},{1,3},{2,0},{3,1},{4,6},{5,7},{6,4},{7,5},{8,10},{9,11},{10,... | collective-permute-start | bytes 1769480 | tf_op jit(solution)/shard_map/ppermute | solution.py:323
  544.6 48.6 %collective-permute-start.48 = (bf16[768,384]{1,0:T(8,128)(2,1)S(1)}, bf16[768,384]{1,0:T(8,128)(2,1)S(1)}, u32[]{:S(2)}, u32[]{:S(2)}) collective-permute-start(bf16[768,384]{1,0:T(8,128)(2,1)S(1)} %add_convert_fusion.11), channel_id=1, source_target_pairs={{0,2},{1,3},{2,0},{3,1},{4,6},{5,7},{6,4},{7,5},{8,10},{9,11},{10,... | collective-permute-start | bytes 1769480 | tf_op jit(solution)/shard_map/ppermute | solution.py:323
  (88 other events, 713.4 us)
where the time goes:
time: 599 us; the launch traced here: 595 us
  waiting for transfers between devices  245 us (41%)
  Pallas kernels  141 us (24%)
  matrix products  106 us (18%)
  starting transfers between devices  50.2 us (8%)
  other arithmetic  26.1 us (4%)
  local copies, waits for them, and re-layouts  24.2 us (4%)
    ppermute x47, waiting for transfers between devices, flip(): return lax.ppermute(value, axis, [(i, i ^ bit) for i in range(size)])  205 us
    pallas_call x10, Pallas kernels, in_parts(): pl.pallas_call(body, grid=(step, grid_rows), in_specs=[moved(spec) for sp...  116 us
    dot_general x30, matrix products, dot(): lax.dot_general(left, right, (contract, ((), ())), preferred_element_type...  106 us
    ppermute x47, starting transfers between devices, flip(): return lax.ppermute(value, axis, [(i, i ^ bit) for i in range(size)])  44.1 us
    pallas_call x4, Pallas kernels, spread(): pl.pallas_call(functools.partial(spread_kernel, r, count, tuple((x.shape[...  24.3 us
    ppermute x1, waiting for transfers between devices, layer(): moved = lax.ppermute(tokens, 'row', [(0, 2), (1, 3)])  21.1 us
    ppermute x1, waiting for transfers between devices, layer(): back = lax.ppermute(mine.astype(bf16), 'row', [(2, 0), (3, 1)]).astype(f32)  19.7 us
    unnamed x163, local copies, waits for them, and re-layouts  15.9 us
  transfers between devices with their start and end apart: 49, of which 22 were waited for; matrix products, arithmetic and copies ran while one was open for 9% of the time, Pallas kernels for 6%

commit v1 on v0

--- a/solution.py
+++ b/solution.py
@@ -316,6 +316,38 @@
         [pltpu.VMEM((PAIR, keys), f32), pltpu.VMEM((PAIR, keys), f32)],
         rows // CONT, lambda w: cost(rows, keys, w, 5),
     )
+
+
+def up_kernel(a_ref, w_ref, g_ref, slope_ref):
+    u = nt(a_ref[...], w_ref[...])
+    share = 0.5 * (1.0 + lax.erf(u * 0.7071067811865476))
+    density = jnp.exp2(u * u * (-0.5 * LOG2E)) * 0.3989422804014327
+    g_ref[...] = (u * share).astype(bf16)
+    slope_ref[...] = (share + u * density).astype(bf16)
+
+
+def feed_up(a, w):
+    rows, width = a.shape
+    hidden = w.shape[0]
+    block = 512
+    out = pl.BlockSpec((rows, block), lambda i: (0, i))
+    return pl.pallas_call(
+        up_kernel,
+        grid=(hidden // block,),
+        in_specs=[
+            pl.BlockSpec((rows, width), lambda i: (0, 0)),
+            pl.BlockSpec((block, width), lambda i: (i, 0)),
+        ],
+        out_specs=[out, out],
+        out_shape=[sds(rows, hidden, bf16)] * 2,
+        compiler_params=pltpu.CompilerParams(vmem_limit_bytes=40 * 2**20),
+        cost_estimate=pl.CostEstimate(
+            flops=2 * rows * width * hidden,
+            transcendentals=2 * rows * hidden,
+            bytes_accessed=2 * (hidden * width + rows * width + 2 * rows * hidden),
+        ),
+        name="feed_up",
+    )(a, w)
 
 
 def flip(value, axis, bit):
@@ -524,6 +556,133 @@
     return value
 
 
+def finish_kernel(
+    gq_ref, gk_ref, gv_ref, part_ref, gains_ref,
+    q_out, k_out, v_out, back_out, gains_out,
+    c_recv, c_part, y_send, y_recv, y_keep, x_send, x_recv, z_send, z_recv,
+    p_send, p_recv, g_send, g_recv, send_sem, recv_sem,
+):
+    grads = (gq_ref, gk_ref, gv_ref)
+    outs = (q_out, k_out, v_out)
+    me, place, depth = lax.axis_index("row"), lax.axis_index("col"), lax.axis_index("dp")
+    core = {"row": me + 1 - 2 * lax.rem(me, 2)}
+    across_x = {"row": lax.rem(me + 2, 4)}
+    across_y = {"col": 1 - place}
+    near_z = {"dp": depth + 1 - 2 * lax.rem(depth, 2)}
+    far_z = {"dp": lax.rem(depth + 2, 4)}
+    partners = (core, across_y, across_x, near_z, far_z)
+    half = gq_ref.shape[0] // 2
+    r = half // 2
+    lanes = gq_ref.shape[1] // 2
+    rows = back_out.shape[0]
+    mine = pl.ds(pl.multiple_of(place * lanes, 128), lanes)
+    theirs = pl.ds(pl.multiple_of((1 - place) * lanes, 128), lanes)
+
+    barrier = pltpu.get_barrier_semaphore()
+    for partner in partners:
+        pl.semaphore_signal(barrier, inc=1, device_id=partner, device_id_type=pl.DeviceIdType.MESH)
+    pl.semaphore_wait(barrier, len(partners))
+    started = []
+
+    def send(source, target, partner):
+        n = len(started)
+        copy = pltpu.make_async_remote_copy(
+            src_ref=source, dst_ref=target, send_sem=send_sem.at[n], recv_sem=recv_sem.at[n],
+            device_id=partner, device_id_type=pl.DeviceIdType.MESH,
+        )
+        copy.start()
+        started.append(copy)
+        return copy
+
+    gain = send(gains_ref, g_recv.at[0], core)
+    part = send(part_ref.at[pl.ds(rows, rows)], c_part, core)
+    hops = [
+        send(g.at[pl.ds(half, half)], c_recv.at[w], core) for w, g in enumerate(grads)
+    ]
+
+    def pass_gain(copy, n, value, partner):
+        copy.wait_recv()
+        value = value + g_recv[n]
+        g_send[n] = value
+        return value, send(g_send.at[n], g_recv.at[n + 1], partner)
+
+    total, gain = pass_gain(gain, 0, gains_ref[...], across_y)
+    part.wait_recv()
+    p_send[...] = (part_ref[0:rows, :].astype(f32) + c_part[...].astype(f32)).astype(bf16)
+    for w, g in enumerate(grads):
+        hops[w].wait_recv()
+        y_send[w] = (
+            g[0:half, theirs].astype(f32) + c_recv[w, :, theirs].astype(f32)
+        ).astype(bf16)
+        hops[w] = send(y_send.at[w], y_recv.at[w], across_y)
+        if w == 0:
+            part = send(p_send, p_recv, across_x)
+        y_keep[w] = g[0:half, mine].astype(f32) + c_recv[w, :, mine].astype(f32)
+    total, gain = pass_gain(gain, 1, total, across_x)
+    for w in range(3):
+        hops[w].wait_recv()
+        x_send[w] = (y_keep[w, r:half, :] + y_recv[w, r:half, :].astype(f32)).astype(bf16)
+        hops[w] = send(x_send.at[w], x_recv.at[w], across_x)
+        y_keep[w, 0:r, :] = y_keep[w, 0:r, :] + y_recv[w, 0:r, :].astype(f32)
+    part.wait_recv()
+    keep = jnp.where(me < 2, 1.0, 0.0)
+    back_out[...] = keep * (p_send[...].astype(f32) + p_recv[...].astype(f32))
+    total, gain = pass_gain(gain, 2, total, near_z)
+    for w in range(3):
+        hops[w].wait_recv()
+        z_send[0, w] = (y_keep[w, 0:r, :] + x_recv[w].astype(f32)).astype(bf16)
+        hops[w] = send(z_send.at[0, w], z_recv.at[0, w], near_z)
+    total, gain = pass_gain(gain, 3, total, far_z)
+    for w in range(3):
+        hops[w].wait_recv()
+        z_send[1, w] = (z_send[0, w].astype(f32) + z_recv[0, w].astype(f32)).astype(bf16)
+        hops[w] = send(z_send.at[1, w], z_recv.at[1, w], far_z)
+    gain.wait_recv()
+    gains_out[...] = total + g_recv[4]
+    for w in range(3):
+        hops[w].wait_recv()
+        outs[w][...] = z_send[1, w].astype(f32) + z_recv[1, w].astype(f32)
+    for copy in started:
+        copy.wait_send()
+
+
+def finish(grads, part, gains):
+    full, width = grads[0].shape
+    half, r, lanes = full // 2, full // 4, width // 2
+    rows = part.shape[0] // 2
+    count = 5 * 4 + 2
+    return pl.pallas_call(
+        finish_kernel,
+        out_shape=[sds(r, lanes, f32)] * 3 + [sds(rows, width, f32), sds(8, width, f32)],
+        in_specs=[pl.BlockSpec(memory_space=pltpu.VMEM)] * 5,
+        out_specs=[pl.BlockSpec(memory_space=pltpu.VMEM)] * 5,
+        scratch_shapes=[
+            pltpu.VMEM((3, half, width), bf16),
+            pltpu.VMEM((rows, width), bf16),
+            pltpu.VMEM((3, half, lanes), bf16),
+            pltpu.VMEM((3, half, lanes), bf16),
+            pltpu.VMEM((3, half, lanes), f32),
+            pltpu.VMEM((3, r, lanes), bf16),
+            pltpu.VMEM((3, r, lanes), bf16),
+            pltpu.VMEM((2, 3, r, lanes), bf16),
+            pltpu.VMEM((2, 3, r, lanes), bf16),
+            pltpu.VMEM((rows, width), bf16),
+            pltpu.VMEM((rows, width), bf16),
+            pltpu.VMEM((4, 8, width), f32),
+            pltpu.VMEM((5, 8, width), f32),
+            pltpu.SemaphoreType.DMA((count,)),
+            pltpu.SemaphoreType.DMA((count,)),
+        ],
+        compiler_params=pltpu.CompilerParams(
+            collective_id=5, has_side_effects=True, vmem_limit_bytes=40 * 2**20
+        ),
+        cost_estimate=pl.CostEstimate(
+            flops=0, transcendentals=0, bytes_accessed=100 * 2**20
+        ),
+        name="finish",
+    )(*grads, part, gains)
+
+
 def layer(
     tokens,
     encoded,
@@ -608,8 +767,7 @@
     (w_down,) = spread(blocks_f, rf, (), 4)
     n3, z3 = unit_rows(h2)
     a3 = (n3 * gain_hidden).astype(bf16)
-    u = nt(a3, w_up)
-    g = jax.nn.gelu(u, approximate=False).astype(bf16)
+    g, slope = feed_up(a3, w_up)
     h3 = h2 + nn(g, w_down)
     n4, z4 = unit_rows(h3)
     layer_out = (n4 * gain_final).astype(bf16)
@@ -620,17 +778,16 @@
     db3 = dh3.astype(bf16)
     g_down = tn(g, db3, bf16)
     (s_down,) = reduce_weights([g_down])
-    _, gelu_pull = jax.vjp(lambda t: jax.nn.gelu(t, approximate=False), u)
     through = nt(db3, w_down)
-    du = gelu_pull(through)[0].astype(bf16)
+    du = (through * slope.astype(f32)).astype(bf16)
     g_up = tn(du, a3, bf16)
-    (s_up,) = reduce_weights([g_up])
     da3 = nn(du, w_up)
     gain_3 = jnp.sum(da3 * n3, axis=0)
     dh2 = dh3 + norm_back(n3, z3, gain_hidden, da3)
     db2 = dh2.astype(bf16)
 
     g_co = tn(oc, db2, bf16)
+    s_up, s_co = reduce_weights([g_up, g_co])
     doc = nt(db2, w_co, bf16)
     dcq, dck, dcv = cross_attention_back(cq, doc, oc, lse_c, ck, cv, at_cross, frames, 3)
     g_cq = tn(dcq, a2, bf16)
@@ -647,7 +804,7 @@
     db1 = dh1.astype(bf16)
 
     g_o = tn(o, db1, bf16)
-    s_o, s_cq, s_ck, s_cv, s_co = reduce_weights([g_o, g_cq, g_ck, g_cv, g_co])
+    s_o, s_cq, s_ck, s_cv = reduce_weights([g_o, g_cq, g_ck, g_cv])
     do = nt(db1, w_o, bf16)
     dq, dk, dv = self_attention_back(q, do, o, lse, k, v, at_self, lim, 3)
     da_all = nn(dk, w_k) + nn(dv, w_v)
@@ -655,15 +812,23 @@
     part = da_all[:ctx]
     own = nn(dq, w_q) + da_all[ctx:]
     gain_1 = jnp.sum(own * n1, axis=0) + jnp.sum(part * n1_context, axis=0)
-    mine = part[: ctx // 2]
-    mine = mine + flip(part[ctx // 2 :].astype(bf16), "row", 1).astype(f32)
-    back = lax.ppermute(mine.astype(bf16), "row", [(2, 0), (3, 1)]).astype(f32)
-    gains = sum_all(jnp.stack([gain_1, gain_2, gain_3, gain_4]))
+    part = part.astype(bf16)
+    gains = jnp.stack([gain_1, gain_2, gain_3, gain_4])
     g_q = tn(dq, a1, bf16)
     g_k = tn(dk, a1_all, bf16)
     g_v = tn(dv, a1_all, bf16)
-    s_q, s_k, s_v = reduce_weights([g_q, g_k, g_v])
-    da1 = own + jnp.where(row < 2, mine + back, 0.0)
+    sizes = (lax.axis_size("row"), lax.axis_size("col"), lax.axis_size("dp"))
+    if sizes == (4, 2, 4):
+        s_q, s_k, s_v, back, gains = finish(
+            (g_q, g_k, g_v), part, jnp.pad(gains, ((0, 4), (0, 0)))
+        )
+    else:
+        mine = part[: ctx // 2].astype(f32) + flip(part[ctx // 2 :], "row", 1).astype(f32)
+        back = lax.ppermute(mine.astype(bf16), "row", [(2, 0), (3, 1)]).astype(f32)
+        back = jnp.where(row < 2, mine + back, 0.0)
+        gains = sum_all(gains)
+        s_q, s_k, s_v = reduce_weights([g_q, g_k, g_v])
+    da1 = own + back
     grad_tokens = dh1 + norm_back(n1, z1, gain_self, da1)
 
     return (

time: 599 us -> 587 us (0.980)
  Pallas kernels: 141 us -> 206 us
  waiting for transfers between devices: 245 us -> 205 us
  matrix products: 106 us -> 75.2 us
  starting transfers between devices: 50.2 us -> 33.9 us
    pallas_call x0 -> x2, Pallas kernels: none -> 65.1 us  [the longest x1 58.9 us: finish(): pl.pallas_call(finish_kernel, out_shape=[sds(r, lanes, f32)] * 3 + [sds(r...]
    dot_general x30 -> x29, matrix products: 106 us -> 75.2 us  [dot(): lax.dot_general(left, right, (contract, ((), ())), preferred_element_type...]
    ppermute x47 -> x34, waiting for transfers between devices: 205 us -> 184 us  [flip(): return lax.ppermute(value, axis, [(i, i ^ bit) for i in range(size)])]
    ppermute x1 -> x0, waiting for transfers between devices: 19.7 us -> none  [layer(): back = lax.ppermute(mine.astype(bf16), 'row', [(2, 0), (3, 1)]).astype(f32)]
    ppermute x47 -> x34, starting transfers between devices: 44.1 us -> 29.2 us  [flip(): return lax.ppermute(value, axis, [(i, i ^ bit) for i in range(size)])]
    unnamed x163 -> x179, local copies, waits for them, and re-layouts: 15.9 us -> 18.5 us
  transfers between devices with their start and end apart: 49 -> 35, of which waited for: 22 -> 12; matrix products, arithmetic and copies ran while one was open for 9% -> 8% of each run, Pallas kernels for 6% -> 17%
where the time goes in v1:
time: 587 us; the launch traced here: 583 us
  Pallas kernels  206 us (35%)
  waiting for transfers between devices  205 us (35%)
  matrix products  75.2 us (13%)
  starting transfers between devices  33.9 us (6%)
  other arithmetic  32 us (5%)
  local copies, waits for them, and re-layouts  27.6 us (5%)
    ppermute x34, waiting for transfers between devices, flip(): return lax.ppermute(value, axis, [(i, i ^ bit) for i in range(size)])  184 us
    pallas_call x10, Pallas kernels, in_parts(): pl.pallas_call(body, grid=(step, grid_rows), in_specs=[moved(spec) for sp...  116 us
    dot_general x29, matrix products, dot(): lax.dot_general(left, right, (contract, ((), ())), preferred_element_type...  75.2 us
    pallas_call x1, Pallas kernels, finish(): pl.pallas_call(finish_kernel, out_shape=[sds(r, lanes, f32)] * 3 + [sds(r...  58.9 us
    ppermute x34, starting transfers between devices, flip(): return lax.ppermute(value, axis, [(i, i ^ bit) for i in range(size)])  29.2 us
    pallas_call x4, Pallas kernels, spread(): pl.pallas_call(functools.partial(spread_kernel, r, count, tuple((x.shape[...  24.3 us
    ppermute x1, waiting for transfers between devices, layer(): moved = lax.ppermute(tokens, 'row', [(0, 2), (1, 3)])  21.1 us
    unnamed x179, local copies, waits for them, and re-layouts  18.5 us
  transfers between devices with their start and end apart: 35, of which 12 were waited for; matrix products, arithmetic and copies ran while one was open for 8% of the time, Pallas kernels for 17%

profile of v1, /device:TPU:0, one launch (start us, length us, event | category | flops | bytes accessed | tf_op | source)
XLA Modules:
  0.0 582.5 jit_solution(8412774012856127263)
XLA Ops:
  9.6 4.8 collective-permute-start.3
  25.1 21.1 %collective-permute-done.3 = bf16[512,768]{1,0:T(8,128)(2,1)} collective-permute-done((bf16[512,768]{1,0:T(8,128)(2,1)}, bf16[512,768]{1,0:T(8,128)(2,1)}, u32[]{:S(2)}, u32[]{:S(2)}) %collective-permute-start.3) | collective-permute-done | bytes 786464 | tf_op jit(solution)/shard_map/ppermute | solution.py:714
  52.1 5.6 shard_map.305
  73.0 8.7 %collective-permute-done.5.refs_2_ = bf16[960,384]{1,0:T(8,128)(2,1)S(1)} collective-permute-done((bf16[960,384]{1,0:T(8,128)(2,1)S(1)}, bf16[960,384]{1,0:T(8,128)(2,1)S(1)}, u32[]{:S(2)}, u32[]{:S(2)}) %collective-permute-start.5) | collective-permute-done | bytes 737312 | tf_op jit(solution)/shard_map/ppermute | solution.py:355
  84.5 10.9 %shard_map.306 = (bf16[512,768]{1,0:T(8,128)(2,1)}, f32[512,768]{1,0:T(8,128)}) custom-call(bf16[512,768]{1,0:T(8,128)(2,1)} %convolution_convert_fusion.17.refs_0_, bf16[1536,768]{1,0:T(8,128)(2,1)} %convolution_convert_fusion.5.refs_1_.refs_3_.refs_4_.refs_6_, bf16[1536,768]{1,0:T(8,128)(2,1)} %convolution_convert_fusion.4.refs_2_.refs_4_.refs_5_.refs_7_, ...), custom_call_target="tpu_custom_call" | custom-call | flops 4026531840 | bytes 5505024 | tf_op jit(solution)/shard_map/pallas_call | solution.py:236
  95.4 11.0 %shard_map.307 = (bf16[512,768]{1,0:T(8,128)(2,1)}, f32[512,768]{1,0:T(8,128)}) custom-call(bf16[512,768]{1,0:T(8,128)(2,1)} %convolution_convert_fusion.17.refs_0_, bf16[1536,768]{1,0:T(8,128)(2,1)} %convolution_convert_fusion.5.refs_1_.refs_3_.refs_4_.refs_6_, ...), custom_call_target="tpu_custom_call", output_to_operand_aliasing={{0}: (7, {}), {1}: (8, {})} | custom-call | flops 4026531840 | bytes 5505024 | tf_op jit(solution)/shard_map/pallas_call | solution.py:236
  107.5 4.7 shard_map.311.w_ref
  112.3 5.7 shard_map.312
  120.2 8.2 %shard_map.308 = (bf16[768,768]{1,0:T(8,128)(2,1)S(1)}, bf16[768,768]{1,0:T(8,128)(2,1)S(1)}, bf16[768,768]{1,0:T(8,128)(2,1)S(1)}, bf16[768,768]{1,0:T(8,128)(2...) custom-call(bf16[960,384]{1,0:T(8,128)(2,1)S(1)} %pack.4.refs_0_, ...), custom_call_target="tpu_custom_call" | custom-call | bytes 8847360 | tf_op jit(solution)/shard_map/pallas_call | solution.py:496
  140.0 11.3 %shard_map.309 = (bf16[512,768]{1,0:T(8,128)(2,1)}, f32[512,768]{1,0:T(8,128)}) custom-call(bf16[512,768]{1,0:T(8,128)(2,1)} %convolution_convert_fusion.16.refs_0_, bf16[1536,768]{1,0:T(8,128)(2,1)} %convolution_convert_fusion.3.refs_1_.refs_4_, bf16[1536,768]{1,0:T(8,128)(2,1)} %convolution_convert_fusion.2.refs_2_.refs_5_, ...), custom_call_target="tpu_custom_call" | custom-call | flops 4831838208 | bytes 6291456 | tf_op jit(solution)/shard_map/pallas_call | solution.py:236
  151.3 11.3 %shard_map.310 = (bf16[512,768]{1,0:T(8,128)(2,1)}, f32[512,768]{1,0:T(8,128)}) custom-call(bf16[512,768]{1,0:T(8,128)(2,1)} %convolution_convert_fusion.16.refs_0_, bf16[1536,768]{1,0:T(8,128)(2,1)} %convolution_convert_fusion.3.refs_1_.refs_4_, ...), custom_call_target="tpu_custom_call", output_to_operand_aliasing={{0}: (4, {}), {1}: (5, {})} | custom-call | flops 4831838208 | bytes 6291456 | tf_op jit(solution)/shard_map/pallas_call | solution.py:236
  166.0 6.2 %feed_up.1 = (bf16[512,3072]{1,0:T(8,128)(2,1)S(1)}, bf16[512,3072]{1,0:T(8,128)(2,1)S(1)}) custom-call(bf16[512,768]{1,0:T(8,128)(2,1)S(1)} %multiply_convert_fusion.2.a_ref, bf16[3072,768]{1,0:T(8,128)(2,1)S(1)} %shard_map.311.w_ref), custom_call_target="tpu_custom_call" | custom-call | flops 2415919104 | bytes 11796480 | tf_op jit(solution)/shard_map/feed_up/pallas_call | solution.py:334
  176.9 5.1 convolution_convert_fusion
  188.0 4.3 convolution_convert_fusion.1
  196.9 11.7 %shard_map.313 = (bf16[512,768]{1,0:T(8,128)(2,1)}, bf16[1536,768]{1,0:T(8,128)(2,1)}, bf16[1536,768]{1,0:T(8,128)(2,1)}) custom-call(bf16[512,768]{1,0:T(8,128)(2,1)} %convolution_convert_fusion.16.refs_0_, bf16[512,768]{1,0:T(8,128)(2,1)} %convolution_convert_fusion.15.refs_1_, bf16[512,768]{1,0:T(8,128)(2,1)} %get-tuple-element.74.refs_2_, ...), custom_call_target="tpu_custom_call" | custom-call | flops 8053063680 | bytes 4194304 | tf_op jit(solution)/shard_map/pallas_call | solution.py:236
  208.6 11.6 %shard_map.314 = (bf16[512,768]{1,0:T(8,128)(2,1)}, bf16[1536,768]{1,0:T(8,128)(2,1)}, bf16[1536,768]{1,0:T(8,128)(2,1)}) custom-call(bf16[512,768]{1,0:T(8,128)(2,1)} %convolution_convert_fusion.16.refs_0_, bf16[512,768]{1,0:T(8,128)(2,1)} %convolution_convert_fusion.15.refs_1_, ...), custom_call_target="tpu_custom_call", output_to_operand_aliasing={{0}: (7, {}), {1}: (8, {}), {2}: (9, {})} | custom-call | flops 8053063680 | bytes 4194304 | tf_op jit(solution)/shard_map/pallas_call | solution.py:236
  220.3 12.0 %shard_map.315 = (bf16[512,768]{1,0:T(8,128)(2,1)}, bf16[1536,768]{1,0:T(8,128)(2,1)}, bf16[1536,768]{1,0:T(8,128)(2,1)}) custom-call(bf16[512,768]{1,0:T(8,128)(2,1)} %convolution_convert_fusion.16.refs_0_, bf16[512,768]{1,0:T(8,128)(2,1)} %convolution_convert_fusion.15.refs_1_, ...), custom_call_target="tpu_custom_call", output_to_operand_aliasing={{0}: (7, {}), {1}: (8, {}), {2}: (9, {})} | custom-call | flops 8053063680 | bytes 4194304 | tf_op jit(solution)/shard_map/pallas_call | solution.py:236
  244.4 4.3 fusion.48
  248.7 11.8 %shard_map.316 = (bf16[512,768]{1,0:T(8,128)(2,1)}, bf16[1536,768]{1,0:T(8,128)(2,1)}, bf16[1536,768]{1,0:T(8,128)(2,1)}) custom-call(bf16[512,768]{1,0:T(8,128)(2,1)} %convolution_convert_fusion.17.refs_0_, bf16[512,768]{1,0:T(8,128)(2,1)} %convolution_convert_fusion.14.refs_1_, bf16[512,768]{1,0:T(8,128)(2,1)} %get-tuple-element.66.refs_2_, ...), custom_call_target="tpu_custom_call" | custom-call | flops 6710886400 | bytes 3670016 | tf_op jit(solution)/shard_map/pallas_call | solution.py:236
  260.5 11.9 %shard_map.317 = (bf16[512,768]{1,0:T(8,128)(2,1)}, bf16[1536,768]{1,0:T(8,128)(2,1)}, bf16[1536,768]{1,0:T(8,128)(2,1)}) custom-call(bf16[512,768]{1,0:T(8,128)(2,1)} %convolution_convert_fusion.17.refs_0_, bf16[512,768]{1,0:T(8,128)(2,1)} %convolution_convert_fusion.14.refs_1_, ...), custom_call_target="tpu_custom_call", output_to_operand_aliasing={{0}: (10, {}), {1}: (11, {}), {2}: (12, {})} | custom-call | flops 6710886400 | bytes 3670016 | tf_op jit(solution)/shard_map/pallas_call | solution.py:236
  272.4 12.2 %shard_map.318 = (bf16[512,768]{1,0:T(8,128)(2,1)}, bf16[1536,768]{1,0:T(8,128)(2,1)}, bf16[1536,768]{1,0:T(8,128)(2,1)}) custom-call(bf16[512,768]{1,0:T(8,128)(2,1)} %convolution_convert_fusion.17.refs_0_, bf16[512,768]{1,0:T(8,128)(2,1)} %convolution_convert_fusion.14.refs_1_, ...), custom_call_target="tpu_custom_call", output_to_operand_aliasing={{0}: (10, {}), {1}: (11, {}), {2}: (12, {})} | custom-call | flops 6710886400 | bytes 3670016 | tf_op jit(solution)/shard_map/pallas_call | solution.py:236
  284.7 4.6 convolution_convert_fusion.12.gv_ref
  311.8 58.9 %finish.1 = (f32[192,384]{1,0:T(8,128)S(1)}, f32[192,384]{1,0:T(8,128)S(1)}, f32[192,384]{1,0:T(8,128)S(1)}, f32[512,768]{1,0:T(8,128)S(1)}, f32[8,768]{1,0:T(8,128)S(1)}) custom-call(bf16[768,768]{1,0:T(8,128)(2,1)S(1)} %convolution_convert_fusion.9.gq_ref, bf16[768,768]{1,0:T(8,128)(2,1)S(1)} %convolution_convert_fusion.13.gk_ref, ...), custom_call_target="tpu_custom_call" | custom-call | bytes 104857600 | tf_op jit(solution)/shard_map/finish/pallas_call | solution.py:654
  389.7 19.0 %collective-permute-done.20 = bf16[1536,384]{1,0:T(8,128)(2,1)S(1)} collective-permute-done((bf16[1536,384]{1,0:T(8,128)(2,1)S(1)}, bf16[1536,384]{1,0:T(8,128)(2,1)S(1)}, u32[]{:S(2)}, u32[]{:S(2)}) %collective-permute-start.20) | collective-permute-done | bytes 1179680 | tf_op jit(solution)/shard_map/ppermute | solution.py:355
  409.3 24.7 %collective-permute-done.31 = bf16[1536,384]{1,0:T(8,128)(2,1)S(1)} collective-permute-done((bf16[1536,384]{1,0:T(8,128)(2,1)S(1)}, bf16[1536,384]{1,0:T(8,128)(2,1)S(1)}, u32[]{:S(2)}, u32[]{:S(2)}) %collective-permute-start.31) | collective-permute-done | bytes 1179680 | tf_op jit(solution)/shard_map/ppermute | solution.py:355
  434.6 30.4 %collective-permute-done.26 = bf16[1920,384]{1,0:T(8,128)(2,1)S(1)} collective-permute-done((bf16[1920,384]{1,0:T(8,128)(2,1)S(1)}, bf16[1920,384]{1,0:T(8,128)(2,1)S(1)}, u32[]{:S(2)}, u32[]{:S(2)}) %collective-permute-start.26) | collective-permute-done | bytes 1474592 | tf_op jit(solution)/shard_map/ppermute | solution.py:355
  470.3 14.7 %collective-permute-done.27 = bf16[960,384]{1,0:T(8,128)(2,1)S(1)} collective-permute-done((bf16[960,384]{1,0:T(8,128)(2,1)S(1)}, bf16[960,384]{1,0:T(8,128)(2,1)S(1)}, u32[]{:S(2)}, u32[]{:S(2)}) %collective-permute-start.27) | collective-permute-done | bytes 737312 | tf_op jit(solution)/shard_map/ppermute | solution.py:355
  488.1 8.1 %collective-permute-done.15 = bf16[384,768]{1,0:T(8,128)(2,1)S(1)} collective-permute-done((bf16[384,768]{1,0:T(8,128)(2,1)S(1)}, bf16[384,768]{1,0:T(8,128)(2,1)S(1)}, u32[]{:S(2)}, u32[]{:S(2)}) %collective-permute-start.15) | collective-permute-done | bytes 589856 | tf_op jit(solution)/shard_map/ppermute | solution.py:355
  497.4 10.1 %collective-permute-done.33 = bf16[768,384]{1,0:T(8,128)(2,1)S(1)} collective-permute-done((bf16[768,384]{1,0:T(8,128)(2,1)S(1)}, bf16[768,384]{1,0:T(8,128)(2,1)S(1)}, u32[]{:S(2)}, u32[]{:S(2)}) %collective-permute-start.33) | collective-permute-done | bytes 589856 | tf_op jit(solution)/shard_map/ppermute | solution.py:355
  507.8 15.2 %collective-permute-done.28 = bf16[960,384]{1,0:T(8,128)(2,1)S(1)} collective-permute-done((bf16[960,384]{1,0:T(8,128)(2,1)S(1)}, bf16[960,384]{1,0:T(8,128)(2,1)S(1)}, u32[]{:S(2)}, u32[]{:S(2)}) %collective-permute-start.28) | collective-permute-done | bytes 737312 | tf_op jit(solution)/shard_map/ppermute | solution.py:355
  524.4 38.8 %collective-permute-done.34 = bf16[768,384]{1,0:T(8,128)(2,1)S(1)} collective-permute-done((bf16[768,384]{1,0:T(8,128)(2,1)S(1)}, bf16[768,384]{1,0:T(8,128)(2,1)S(1)}, u32[]{:S(2)}, u32[]{:S(2)}) %collective-permute-start.34) | collective-permute-done | bytes 589856 | tf_op jit(solution)/shard_map/ppermute | solution.py:355
  564.4 13.4 %collective-permute-done.29 = bf16[960,384]{1,0:T(8,128)(2,1)S(1)} collective-permute-done((bf16[960,384]{1,0:T(8,128)(2,1)S(1)}, bf16[960,384]{1,0:T(8,128)(2,1)S(1)}, u32[]{:S(2)}, u32[]{:S(2)}) %collective-permute-start.29) | collective-permute-done | bytes 737312 | tf_op jit(solution)/shard_map/ppermute | solution.py:355
  (367 shorter events, 147.7 us)
Async XLA Ops:
  4.1 16.2 %collective-permute-start.1 = (bf16[576,384]{1,0:T(8,128)(2,1)S(1)}, bf16[576,384]{1,0:T(8,128)(2,1)S(1)}, u32[]{:S(2)}, u32[]{:S(2)}) collective-permute-start(bf16[576,384]{1,0:T(8,128)(2,1)S(1)} %pack.3.refs_0_), channel_id=1, source_target_pairs={{0,16},{8,24},{16,0},{24,8},{1,17},{9,25},{17,1},{25,9},{2,18},{10... | collective-permute-start | bytes 1327112 | tf_op jit(solution)/shard_map/ppermute | solution.py:355
  7.2 41.8 %collective-permute-start = (bf16[576,384]{1,0:T(8,128)(2,1)S(1)}, bf16[576,384]{1,0:T(8,128)(2,1)}, u32[]{:S(2)}, u32[]{:S(2)}) collective-permute-start(bf16[576,384]{1,0:T(8,128)(2,1)S(1)} %pack.3.refs_0_), channel_id=1, source_target_pairs={{0,4},{4,0},{1,5},{5,1},{2,6},{6,2},{3,7},{7,3},{8,12},{12,8},{9,1... | collective-permute-start | bytes 1327112 | tf_op jit(solution)/shard_map/ppermute | solution.py:355
  8.9 42.6 %collective-permute-start.9 = (bf16[768,384]{1,0:T(8,128)(2,1)S(1)}, bf16[768,384]{1,0:T(8,128)(2,1)}, u32[]{:S(2)}, u32[]{:S(2)}) collective-permute-start(bf16[768,384]{1,0:T(8,128)(2,1)S(1)} %pack.5.refs_0_), channel_id=1, source_target_pairs={{0,16},{8,24},{16,0},{24,8},{1,17},{9,25},{17,1},{25,9},{2,18},{10... | collective-permute-start | bytes 1769480 | tf_op jit(solution)/shard_map/ppermute | solution.py:355
  9.5 60.0 %collective-permute-start.8 = (bf16[768,384]{1,0:T(8,128)(2,1)S(1)}, bf16[768,384]{1,0:T(8,128)(2,1)}, u32[]{:S(2)}, u32[]{:S(2)}) collective-permute-start(bf16[768,384]{1,0:T(8,128)(2,1)S(1)} %pack.5.refs_0_), channel_id=1, source_target_pairs={{0,4},{4,0},{1,5},{5,1},{2,6},{6,2},{3,7},{7,3},{8,12},{12,8},{9,1... | collective-permute-start | bytes 1769480 | tf_op jit(solution)/shard_map/ppermute | solution.py:355
  9.6 36.6 %collective-permute-start.3 = (bf16[512,768]{1,0:T(8,128)(2,1)}, bf16[512,768]{1,0:T(8,128)(2,1)}, u32[]{:S(2)}, u32[]{:S(2)}) collective-permute-start(bf16[512,768]{1,0:T(8,128)(2,1)} %param.18), channel_id=1, source_target_pairs={{0,16},{8,24},{1,17},{9,25},{2,18},{10,26},{3,19},{11,27},{4,20},{... | collective-permute-start | bytes 2359304 | tf_op jit(solution)/shard_map/ppermute | solution.py:714
  20.4 31.2 %collective-permute-start.2 = (bf16[576,384]{1,0:T(8,128)(2,1)S(1)}, bf16[576,384]{1,0:T(8,128)(2,1)}, u32[]{:S(2)}, u32[]{:S(2)}) collective-permute-start(bf16[576,384]{1,0:T(8,128)(2,1)S(1)} %collective-permute-done.1.refs_2_), channel_id=1, source_target_pairs={{0,4},{4,0},{1,5},{5,1},{2,6},{6,2},{3,7},{7,3},{8,12},{12,8},{9,1... | collective-permute-start | bytes 1327112 | tf_op jit(solution)/shard_map/ppermute | solution.py:355
  46.2 66.1 %collective-permute-start.11 = (bf16[768,384]{1,0:T(8,128)(2,1)}, bf16[768,384]{1,0:T(8,128)(2,1)}, u32[]{:S(2)}, u32[]{:S(2)}) collective-permute-start(bf16[768,384]{1,0:T(8,128)(2,1)} %refs_0_.6), channel_id=1, source_target_pairs={{0,4},{4,0},{1,5},{5,1},{2,6},{6,2},{3,7},{7,3},{8,12},{12,8},{9,1... | collective-permute-start | bytes 1769480 | tf_op jit(solution)/shard_map/ppermute | solution.py:355
  49.0 22.1 %collective-permute-start.12 = (bf16[768,384]{1,0:T(8,128)(2,1)}, bf16[768,384]{1,0:T(8,128)(2,1)}, u32[]{:S(2)}, u32[]{:S(2)}) collective-permute-start(bf16[768,384]{1,0:T(8,128)(2,1)} %refs_0_.6), channel_id=1, source_target_pairs={{0,16},{8,24},{16,0},{24,8},{1,17},{9,25},{17,1},{25,9},{2,18},{10... | collective-permute-start | bytes 1769480 | tf_op jit(solution)/shard_map/ppermute | solution.py:355
  51.5 30.2 %collective-permute-start.5 = (bf16[960,384]{1,0:T(8,128)(2,1)S(1)}, bf16[960,384]{1,0:T(8,128)(2,1)S(1)}, u32[]{:S(2)}, u32[]{:S(2)}) collective-permute-start(bf16[960,384]{1,0:T(8,128)(2,1)S(1)} %pack.4.refs_0_), channel_id=1, source_target_pairs={{0,16},{8,24},{16,0},{24,8},{1,17},{9,25},{17,1},{25,9},{2,18},{10... | collective-permute-start | bytes 2211848 | tf_op jit(solution)/shard_map/ppermute | solution.py:355
  51.6 30.6 %collective-permute-start.10 = (bf16[768,384]{1,0:T(8,128)(2,1)}, bf16[768,384]{1,0:T(8,128)(2,1)S(1)}, u32[]{:S(2)}, u32[]{:S(2)}) collective-permute-start(bf16[768,384]{1,0:T(8,128)(2,1)} %collective-permute-done.9.refs_2_), channel_id=1, source_target_pairs={{0,4},{4,0},{1,5},{5,1},{2,6},{6,2},{3,7},{7,3},{8,12},{12,8},{9,1... | collective-permute-start | bytes 1769480 | tf_op jit(solution)/shard_map/ppermute | solution.py:355
  69.5 50.7 %collective-permute-start.4 = (bf16[960,384]{1,0:T(8,128)(2,1)S(1)}, bf16[960,384]{1,0:T(8,128)(2,1)}, u32[]{:S(2)}, u32[]{:S(2)}) collective-permute-start(bf16[960,384]{1,0:T(8,128)(2,1)S(1)} %pack.4.refs_0_), channel_id=1, source_target_pairs={{0,4},{4,0},{1,5},{5,1},{2,6},{6,2},{3,7},{7,3},{8,12},{12,8},{9,1... | collective-permute-start | bytes 2211848 | tf_op jit(solution)/shard_map/ppermute | solution.py:355
  71.0 49.2 %collective-permute-start.7 = (bf16[384,768]{1,0:T(8,128)(2,1)S(1)}, bf16[384,768]{1,0:T(8,128)(2,1)}, u32[]{:S(2)}, u32[]{:S(2)}) collective-permute-start(bf16[384,768]{1,0:T(8,128)(2,1)S(1)} %pad.8.refs_4_), channel_id=1, source_target_pairs={{0,16},{8,24},{16,0},{24,8},{1,17},{9,25},{17,1},{25,9},{2,18},{10... | collective-permute-start | bytes 1769480 | tf_op jit(solution)/shard_map/ppermute | solution.py:355
  81.7 30.6 %collective-permute-start.13 = (bf16[768,384]{1,0:T(8,128)(2,1)}, bf16[768,384]{1,0:T(8,128)(2,1)}, u32[]{:S(2)}, u32[]{:S(2)}) collective-permute-start(bf16[768,384]{1,0:T(8,128)(2,1)} %collective-permute-done.12.refs_2_), channel_id=1, source_target_pairs={{0,4},{4,0},{1,5},{5,1},{2,6},{6,2},{3,7},{7,3},{8,12},{12,8},{9,1... | collective-permute-start | bytes 1769480 | tf_op jit(solution)/shard_map/ppermute | solution.py:355
  83.0 37.2 %collective-permute-start.6 = (bf16[960,384]{1,0:T(8,128)(2,1)S(1)}, bf16[960,384]{1,0:T(8,128)(2,1)}, u32[]{:S(2)}, u32[]{:S(2)}) collective-permute-start(bf16[960,384]{1,0:T(8,128)(2,1)S(1)} %collective-permute-done.5.refs_2_), channel_id=1, source_target_pairs={{0,4},{4,0},{1,5},{5,1},{2,6},{6,2},{3,7},{7,3},{8,12},{12,8},{9,1... | collective-permute-start | bytes 2211848 | tf_op jit(solution)/shard_map/ppermute | solution.py:355
  301.8 78.6 %collective-permute-start.25 = (bf16[384,768]{1,0:T(8,128)(2,1)}, bf16[384,768]{1,0:T(8,128)(2,1)S(1)}, u32[]{:S(2)}, u32[]{:S(2)}) collective-permute-start(bf16[384,768]{1,0:T(8,128)(2,1)} %slice.260), channel_id=1, source_target_pairs={{0,8},{8,0},{16,24},{24,16},{1,9},{9,1},{17,25},{25,17},{2,10},{10... | collective-permute-start | bytes 1769480 | tf_op jit(solution)/shard_map/ppermute | solution.py:355
  305.2 75.4 %collective-permute-start.30 = (bf16[1536,768]{1,0:T(8,128)(2,1)}, bf16[1536,768]{1,0:T(8,128)(2,1)}, u32[]{:S(2)}, u32[]{:S(2)}) collective-permute-start(bf16[1536,768]{1,0:T(8,128)(2,1)} %slice.271), channel_id=1, source_target_pairs={{0,8},{8,0},{16,24},{24,16},{1,9},{9,1},{17,25},{25,17},{2,10},{10... | collective-permute-start | bytes 7077896 | tf_op jit(solution)/shard_map/ppermute | solution.py:355
  305.4 79.4 %collective-permute-start.24 = (bf16[1536,768]{1,0:T(8,128)(2,1)}, bf16[1536,768]{1,0:T(8,128)(2,1)}, u32[]{:S(2)}, u32[]{:S(2)}) collective-permute-start(bf16[1536,768]{1,0:T(8,128)(2,1)} %slice.257), channel_id=1, source_target_pairs={{0,8},{8,0},{16,24},{24,16},{1,9},{9,1},{17,25},{25,17},{2,10},{10... | collective-permute-start | bytes 7077896 | tf_op jit(solution)/shard_map/ppermute | solution.py:355
  305.8 69.9 %collective-permute-start.17 = (bf16[384,768]{1,0:T(8,128)(2,1)S(1)}, bf16[384,768]{1,0:T(8,128)(2,1)}, u32[]{:S(2)}, u32[]{:S(2)}) collective-permute-start(bf16[384,768]{1,0:T(8,128)(2,1)S(1)} %slice.236), channel_id=1, source_target_pairs={{0,8},{8,0},{16,24},{24,16},{1,9},{9,1},{17,25},{25,17},{2,10},{10... | collective-permute-start | bytes 1769480 | tf_op jit(solution)/shard_map/ppermute | solution.py:355
  306.9 70.2 %collective-permute-start.16 = (bf16[384,768]{1,0:T(8,128)(2,1)}, bf16[384,768]{1,0:T(8,128)(2,1)S(1)}, u32[]{:S(2)}, u32[]{:S(2)}) collective-permute-start(bf16[384,768]{1,0:T(8,128)(2,1)} %slice.233), channel_id=1, source_target_pairs={{0,8},{8,0},{16,24},{24,16},{1,9},{9,1},{17,25},{25,17},{2,10},{10... | collective-permute-start | bytes 1769480 | tf_op jit(solution)/shard_map/ppermute | solution.py:355
  379.8 28.9 %collective-permute-start.20 = (bf16[1536,384]{1,0:T(8,128)(2,1)S(1)}, bf16[1536,384]{1,0:T(8,128)(2,1)S(1)}, u32[]{:S(2)}, u32[]{:S(2)}) collective-permute-start(bf16[1536,384]{1,0:T(8,128)(2,1)S(1)} %broadcast_select_fusion.2), channel_id=1, source_target_pairs={{0,4},{4,0},{1,5},{5,1},{2,6},{6,2},{3,7},{7,3},{8,12},{12,8},{9,1... | collective-permute-start | bytes 3538952 | tf_op jit(solution)/shard_map/ppermute | solution.py:355
  383.2 50.8 %collective-permute-start.31 = (bf16[1536,384]{1,0:T(8,128)(2,1)S(1)}, bf16[1536,384]{1,0:T(8,128)(2,1)S(1)}, u32[]{:S(2)}, u32[]{:S(2)}) collective-permute-start(bf16[1536,384]{1,0:T(8,128)(2,1)S(1)} %broadcast_select_fusion.1), channel_id=1, source_target_pairs={{0,4},{4,0},{1,5},{5,1},{2,6},{6,2},{3,7},{7,3},{8,12},{12,8},{9,1... | collective-permute-start | bytes 3538952 | tf_op jit(solution)/shard_map/ppermute | solution.py:355
  388.0 77.0 %collective-permute-start.26 = (bf16[1920,384]{1,0:T(8,128)(2,1)S(1)}, bf16[1920,384]{1,0:T(8,128)(2,1)S(1)}, u32[]{:S(2)}, u32[]{:S(2)}) collective-permute-start(bf16[1920,384]{1,0:T(8,128)(2,1)S(1)} %broadcast_select_fusion), channel_id=1, source_target_pairs={{0,4},{4,0},{1,5},{5,1},{2,6},{6,2},{3,7},{7,3},{8,12},{12,8},{9,1... | collective-permute-start | bytes 4423688 | tf_op jit(solution)/shard_map/ppermute | solution.py:355
  409.2 56.5 %collective-permute-start.21 = (bf16[768,384]{1,0:T(8,128)(2,1)S(1)}, bf16[768,384]{1,0:T(8,128)(2,1)S(1)}, u32[]{:S(2)}, u32[]{:S(2)}) collective-permute-start(bf16[768,384]{1,0:T(8,128)(2,1)S(1)} %slice.251), channel_id=1, source_target_pairs={{0,16},{8,24},{16,0},{24,8},{1,17},{9,25},{17,1},{25,9},{2,18},{10... | collective-permute-start | bytes 1769480 | tf_op jit(solution)/shard_map/ppermute | solution.py:355
  434.5 33.6 %collective-permute-start.32 = (bf16[768,384]{1,0:T(8,128)(2,1)S(1)}, bf16[768,384]{1,0:T(8,128)(2,1)S(1)}, u32[]{:S(2)}, u32[]{:S(2)}) collective-permute-start(bf16[768,384]{1,0:T(8,128)(2,1)S(1)} %slice.275), channel_id=1, source_target_pairs={{0,16},{8,24},{16,0},{24,8},{1,17},{9,25},{17,1},{25,9},{2,18},{10... | collective-permute-start | bytes 1769480 | tf_op jit(solution)/shard_map/ppermute | solution.py:355
  465.6 19.4 %collective-permute-start.27 = (bf16[960,384]{1,0:T(8,128)(2,1)S(1)}, bf16[960,384]{1,0:T(8,128)(2,1)S(1)}, u32[]{:S(2)}, u32[]{:S(2)}) collective-permute-start(bf16[960,384]{1,0:T(8,128)(2,1)S(1)} %slice.267), channel_id=1, source_target_pairs={{0,16},{8,24},{16,0},{24,8},{1,17},{9,25},{17,1},{25,9},{2,18},{10... | collective-permute-start | bytes 2211848 | tf_op jit(solution)/shard_map/ppermute | solution.py:355
  465.9 19.4 %collective-permute-start.22 = (bf16[768,384]{1,0:T(8,128)(2,1)S(1)}, bf16[768,384]{1,0:T(8,128)(2,1)S(1)}, u32[]{:S(2)}, u32[]{:S(2)}) collective-permute-start(bf16[768,384]{1,0:T(8,128)(2,1)S(1)} %add_convert_fusion.13), channel_id=1, source_target_pairs={{0,1},{1,0},{2,3},{3,2},{4,5},{5,4},{6,7},{7,6},{8,9},{9,8},{10,11... | collective-permute-start | bytes 1769480 | tf_op jit(solution)/shard_map/ppermute | solution.py:355
  466.0 30.2 %collective-permute-start.15 = (bf16[384,768]{1,0:T(8,128)(2,1)S(1)}, bf16[384,768]{1,0:T(8,128)(2,1)S(1)}, u32[]{:S(2)}, u32[]{:S(2)}) collective-permute-start(bf16[384,768]{1,0:T(8,128)(2,1)S(1)} %get-tuple-element.196), channel_id=1, source_target_pairs={{0,16},{8,24},{16,0},{24,8},{1,17},{9,25},{17,1},{25,9},{2,18},{10... | collective-permute-start | bytes 1769480 | tf_op jit(solution)/shard_map/ppermute | solution.py:355
  468.3 39.2 %collective-permute-start.33 = (bf16[768,384]{1,0:T(8,128)(2,1)S(1)}, bf16[768,384]{1,0:T(8,128)(2,1)S(1)}, u32[]{:S(2)}, u32[]{:S(2)}) collective-permute-start(bf16[768,384]{1,0:T(8,128)(2,1)S(1)} %add_convert_fusion.10), channel_id=1, source_target_pairs={{0,1},{1,0},{2,3},{3,2},{4,5},{5,4},{6,7},{7,6},{8,9},{9,8},{10,11... | collective-permute-start | bytes 1769480 | tf_op jit(solution)/shard_map/ppermute | solution.py:355
  485.2 37.8 %collective-permute-start.28 = (bf16[960,384]{1,0:T(8,128)(2,1)S(1)}, bf16[960,384]{1,0:T(8,128)(2,1)S(1)}, u32[]{:S(2)}, u32[]{:S(2)}) collective-permute-start(bf16[960,384]{1,0:T(8,128)(2,1)S(1)} %add_convert_fusion.8), channel_id=1, source_target_pairs={{0,1},{1,0},{2,3},{3,2},{4,5},{5,4},{6,7},{7,6},{8,9},{9,8},{10,11... | collective-permute-start | bytes 2211848 | tf_op jit(solution)/shard_map/ppermute | solution.py:355
  485.5 37.8 %collective-permute-start.23 = (bf16[768,384]{1,0:T(8,128)(2,1)S(1)}, bf16[768,384]{1,0:T(8,128)(2,1)S(1)}, u32[]{:S(2)}, u32[]{:S(2)}) collective-permute-start(bf16[768,384]{1,0:T(8,128)(2,1)S(1)} %add_convert_fusion.12), channel_id=1, source_target_pairs={{0,2},{1,3},{2,0},{3,1},{4,6},{5,7},{6,4},{7,5},{8,10},{9,11},{10,... | collective-permute-start | bytes 1769480 | tf_op jit(solution)/shard_map/ppermute | solution.py:355
  507.6 55.7 %collective-permute-start.34 = (bf16[768,384]{1,0:T(8,128)(2,1)S(1)}, bf16[768,384]{1,0:T(8,128)(2,1)S(1)}, u32[]{:S(2)}, u32[]{:S(2)}) collective-permute-start(bf16[768,384]{1,0:T(8,128)(2,1)S(1)} %add_convert_fusion.9), channel_id=1, source_target_pairs={{0,2},{1,3},{2,0},{3,1},{4,6},{5,7},{6,4},{7,5},{8,10},{9,11},{10,... | collective-permute-start | bytes 1769480 | tf_op jit(solution)/shard_map/ppermute | solution.py:355
  523.2 54.6 %collective-permute-start.29 = (bf16[960,384]{1,0:T(8,128)(2,1)S(1)}, bf16[960,384]{1,0:T(8,128)(2,1)S(1)}, u32[]{:S(2)}, u32[]{:S(2)}) collective-permute-start(bf16[960,384]{1,0:T(8,128)(2,1)S(1)} %add_convert_fusion.7), channel_id=1, source_target_pairs={{0,2},{1,3},{2,0},{3,1},{4,6},{5,7},{6,4},{7,5},{8,10},{9,11},{10,... | collective-permute-start | bytes 2211848 | tf_op jit(solution)/shard_map/ppermute | solution.py:355
  (84 other events, 539.6 us)
